TPU v7x, 128 devices: a whole 4x4x4 slice. The times are simulated.
128 devices in a mesh: lat: 8 (over z, core), lon: 16 (over x, y).
Axes of the slice: x: 4, y: 4, z: 4, core: 2. Of those that a mesh axis runs over, the one named last changes fastest.
Arguments:
- background: bfloat16 [131072, 384], P(('lat', 'lon')), may hold values from -6 to 6
- increment: bfloat16 [131072, 384], P(('lat', 'lon')), may hold values from -6 to 6
- coefficients: bfloat16 [384, 4352], replicated, may hold values from -0.3125 to 0.3125
- departures: bfloat16 [512, 128, 4352], P(('lat', 'lon')), may hold values from -24 to 24
- bias_pred: float32 [512, 128, 8], P(('lat', 'lon')), may hold values from -6 to 6
- beta_incr: float32 [8, 4352], replicated, may hold values from -2 to 2
- obs_weight: float32 [4352], replicated, may hold values from 0.1 to 1
- obs_count: int32 [512], P(('lat', 'lon')), may hold values from 1 to 128
- col_index: int32 [512, 128], P(('lat', 'lon')), may hold values from 0 to 131071, as said below
Outputs:
- radiance: bfloat16 [512, 128, 4352], P(('lat', 'lon'))
- column_grad: bfloat16 [131072, 384], P(('lat', 'lon'))
- bias_grad: float32 [4352, 8], P(('lat', 'lon'))
Inputs may be any that keep to these rules, and one draw needn't show every extreme that they name: `col_index`: column c is owned by the block of 1024 columns c // 1024. Among the 512 slots of the blocks of one device, at most 6 name columns of any one owner, and some owner is named by exactly 6 slots of every device.
All inputs are finite; a program needn't handle non-finite values.
Results may differ from a plain program's by a relative error of at most 0.005.
Values may be sent and summed in bfloat16 or wider, within the bound.
No kernel may reach another device: no remote copies, remote signals or barrier semaphores. Data moves between devices by JAX's collectives and lax.ppermute only.
A program may use at most 128 MiB of HBM per device.

v0:
```python
import jax
import jax.numpy as jnp
from jax import lax
from jax.sharding import Mesh
from jax.sharding import PartitionSpec as P

LAT_LON = ("lat_0", "lat_1", "lon_0", "lon_1")
LAT = ("lat_0", "lat_1")
LON = ("lon_0", "lon_1")


def cut_along(x, dim, count):
    dims = x.shape
    parts = x.reshape(*dims[:dim], count, dims[dim] // count, *dims[dim + 1 :])
    return jnp.moveaxis(parts, dim, 0)


def in_order(parts, dim):
    parts = jnp.moveaxis(parts, 0, dim)
    dims = parts.shape
    return parts.reshape(*dims[:dim], dims[dim] * dims[dim + 1], *dims[dim + 2 :])


def one_exchange(x, axis, axes, splits, concats):
    sizes = [lax.axis_size(a) for a in axes]
    parts = cut_along(x, splits[0], sizes[0])
    parts = jnp.moveaxis(cut_along(parts, splits[1] + 1, sizes[1]), 0, 1)
    inside = parts.shape[2:]
    parts = parts.reshape(-1, *inside)
    parts = lax.all_to_all(parts, axis, split_axis=0, concat_axis=0, tiled=True)
    parts = in_order(parts.reshape(*sizes, *inside), concats[0] + 1)
    return in_order(parts, concats[1])


def own_block(parts, axes, turns):
    dims = [lax.axis_size(a) for a in axes]
    parts = parts.reshape(*dims, *parts.shape[1:])
    parts = parts.transpose(*turns, *range(len(axes), parts.ndim))
    parts = parts.reshape(-1, *parts.shape[len(axes) :])
    for k in turns:
        parts = lax.psum_scatter(parts, axes[k], scatter_dimension=0, tiled=True)
    return parts[0]


def sum_by_axis(x, axes, turns, dim):
    count = lax.axis_size(axes)
    return own_block(cut_along(x, dim, count), axes, turns)


def route_ids(requests, lat_count, lon_count):
    shaped = requests.reshape((lat_count, lon_count) + requests.shape[1:])
    moved = one_exchange(shaped, LAT_LON, (LAT, LON), (0, 1), (0, 1))
    return moved.reshape(requests.shape)


def route_profiles(payload, lat_count, lon_count):
    shaped = payload.reshape((lat_count, lon_count) + payload.shape[1:])
    moved = one_exchange(shaped, LAT_LON, (LAT, LON), (0, 1), (0, 1))
    return moved.reshape(payload.shape)


def route_adjoint(payload, lat_count, lon_count):
    shaped = payload.reshape((lat_count, lon_count) + payload.shape[1:])
    moved = one_exchange(shaped, LAT_LON, (LAT, LON), (0, 1), (0, 1))
    return moved.reshape(payload.shape)


def shards(
    background,
    increment,
    coefficients,
    departures,
    bias_pred,
    beta_incr,
    obs_weight,
    obs_count,
    col_index,
):
    lat_count = lax.axis_size(LAT)
    lon_count = lax.axis_size(LON)
    devices = lat_count * lon_count
    column_count, profile_len = background.shape
    block_count, block_len = col_index.shape
    channels = coefficients.shape[1]
    npredictors = bias_pred.shape[2]
    slot_count = block_count * block_len
    capacity = 3 * slot_count // (2 * devices)
    scaling = 1.0 / jnp.sqrt(jnp.float32(slot_count * devices))
    columns = col_index.reshape(slot_count)
    owners = columns // column_count
    local_cols = columns % column_count
    owner_table = (owners[:, None] == jnp.arange(devices, dtype=jnp.int32)[None, :]).astype(
        jnp.int32
    )
    bucket_rank = jnp.sum(jnp.cumsum(owner_table, axis=0) * owner_table, axis=1) - 1
    position = owners * capacity + bucket_rank
    requests = jnp.zeros((devices * capacity,), jnp.int32).at[position].set(local_cols)
    wanted = route_ids(requests.reshape(devices, capacity), lat_count, lon_count).reshape(
        devices * capacity
    )
    base_rows = background[wanted]
    step_rows = increment[wanted]
    owner_jacobian = 1.0 + 0.5 * jnp.tanh(base_rows.astype(jnp.float32))
    formed_rows = (step_rows.astype(jnp.float32) * owner_jacobian).astype(jnp.bfloat16)
    arrived = route_profiles(
        formed_rows.reshape(devices, capacity, profile_len), lat_count, lon_count
    )
    predictor = arrived.reshape(devices * capacity, profile_len)[position]
    flat_pred = bias_pred.reshape(slot_count, npredictors)
    slot_pos = jnp.arange(block_len, dtype=jnp.int32)
    present = (slot_pos[None, :] < obs_count[:, None]).reshape(slot_count, 1)
    radiance_f = jnp.dot(predictor, coefficients, preferred_element_type=jnp.float32)
    radiance_f = radiance_f + jnp.dot(flat_pred, beta_incr, precision=lax.Precision.HIGHEST)
    radiance_f = jnp.where(present, radiance_f, jnp.float32(0.0))
    radiance = radiance_f.astype(jnp.bfloat16).reshape(block_count, block_len, channels)
    observed = departures.reshape(slot_count, channels).astype(jnp.float32)
    misfit = jnp.where(present, obs_weight[None, :] * (radiance_f - observed), jnp.float32(0.0))
    pulled = lax.dot_general(
        misfit.astype(jnp.bfloat16),
        coefficients,
        (((1,), (1,)), ((), ())),
        preferred_element_type=jnp.float32,
    )
    outgoing = jnp.zeros((devices * capacity, profile_len), jnp.float32).at[position].set(pulled)
    returned = route_adjoint(outgoing.reshape(devices, capacity, profile_len), lat_count, lon_count)
    returned = returned.reshape(devices * capacity, profile_len) * owner_jacobian
    gradient = jnp.zeros((column_count, profile_len), jnp.float32).at[wanted].add(returned)
    column_grad = gradient.astype(jnp.bfloat16)
    local_bias = (
        lax.dot_general(
            misfit, flat_pred, (((0,), (0,)), ((), ())), precision=lax.Precision.HIGHEST
        )
        * scaling
    )
    bias_grad = sum_by_axis(local_bias, LAT_LON, (1, 0, 2, 3), 0)
    return (radiance, column_grad, bias_grad)


def solution(mesh):
    finer = Mesh(mesh.devices.reshape(4, 2, 4, 4), ("lat_0", "lat_1", "lon_0", "lon_1"))
    in_specs = (
        P(LAT_LON, None),
        P(LAT_LON, None),
        P(),
        P(LAT_LON, None, None),
        P(LAT_LON, None, None),
        P(),
        P(),
        P(LAT_LON),
        P(LAT_LON, None),
    )
    out_specs = (P(LAT_LON, None, None), P(LAT_LON, None), P(LAT_LON, None))
    return jax.shard_map(
        shards, mesh=finer, in_specs=in_specs, out_specs=out_specs, check_vma=False
    )
```

profile of v0, /device:TPU:0, one launch (start us, length us, event | category | flops | bytes accessed | tf_op | source)
XLA Modules:
  0.0 221.4 jit_solution(12282315682797657355)
XLA Ops:
  7.2 0.0 copy-start
  7.2 0.8 add_select_fusion.2
  8.0 0.9 add_select_fusion.1
  8.9 0.1 copy.17
  9.0 0.2 fusion.20
  9.2 0.7 copy-done.2
  10.0 1.0 broadcast_add_fusion
  11.0 0.2 fusion.19
  11.2 0.7 compare_select_fusion.1
  11.9 2.4 %scatter_custom_fusion = s32[768]{0:T(1024)S(1)} fusion(s32[512]{0:T(512)S(1)} %bitcast.108, s32[512]{0:T(512)S(1)} %get-tuple-element.3, s32[]{:T(128)} %constant.40.clone.1), kind=kCustom, calls=%fused_computation.64 | custom fusion | bytes 3076 | tf_op jit(solution)/shard_map/scatter | solution.py:97
  14.4 0.1 reshape_transpose_transpose_reshape_reshape_reshape_reshape.7
  14.5 20.5 %all_to_all.15 = s32[128,1,1,6]{3,2,1,0:T(1,128)S(1)} all-to-all(s32[128,1,1,6]{3,2,1,0:T(1,128)S(1)} %bitcast.104), channel_id=1, replica_groups=mesh['lat_0'=4,'lat_1'=2,'lon_0'=4,'lon_1'=4] {'lat_0','lat_1','lon_0','..., dimensions={0} | all-to-all | bytes 6144 | tf_op jit(solution)/shard_map/all_to_all | solution.py:30
  35.0 0.1 reshape_reshape_reshape.9
  35.2 4.3 %gather_fusion.1 = bf16[768,384]{1,0:T(8,128)(2,1)} fusion(bf16[1024,384]{1,0:T(8,128)(2,1)} %param.9, s32[1024]{0:T(1024)S(1)} %pad_clamp_fusion.1), kind=kCustom, calls=%fused_computation.1 | custom fusion | bytes 1182720 | tf_op jit(solution)/shard_map/gather | solution.py:101
  39.5 4.3 %gather_fusion = bf16[768,384]{1,0:T(8,128)(2,1)} fusion(bf16[1024,384]{1,0:T(8,128)(2,1)} %param.10, s32[1024]{0:T(1024)S(1)} %pad_clamp_fusion.1), kind=kCustom, calls=%fused_computation | custom fusion | bytes 1182720 | tf_op jit(solution)/shard_map/gather | solution.py:102
  43.8 2.3 %multiply_convert_fusion = bf16[768,384]{1,0:T(8,128)(2,1)} fusion(bf16[768,384]{1,0:T(8,128)(2,1)} %gather_fusion, bf16[768,384]{1,0:T(8,128)(2,1)} %gather_fusion.1), kind=kLoop, calls=%fused_computation.20 | loop fusion | flops 1769472 | bytes 1769472 | tf_op jit(solution)/shard_map/convert_element_type | solution.py:104
  46.2 2.0 reshape.263
  48.2 5.9 %all-to-all-start.1 = ((bf16[128,1,1,6,384]{4,3,2,1,0:T(8,128)(2,1)}), bf16[128,1,1,6,384]{4,3,2,1,0:T(8,128)(2,1)}, u32[]{:S(2)}, u32[]{:S(2)}) async-start(bf16[128,1,1,6,384]{4,3,2,1,0:T(8,128)(2,1)} %bitcast.99), calls=%async_computation.1 | async-start | bytes 1572864 | tf_op jit(solution)/shard_map/all_to_all | solution.py:30
  54.1 0.1 fusion.30
  54.2 15.7 %all-to-all-done.1 = bf16[128,1,1,6,384]{4,3,2,1,0:T(8,128)(2,1)} async-done(((bf16[128,1,1,6,384]{4,3,2,1,0:T(8,128)(2,1)}), bf16[128,1,1,6,384]{4,3,2,1,0:T(8,128)(2,1)}, u32[]{:S(2)}, u32[]{:S(2)}) %all-to-all-start.1) | async-done | bytes 589856 | tf_op jit(solution)/shard_map/all_to_all | solution.py:30
  69.9 2.0 reshape_reshape_reshape.10
  71.9 3.6 %gather_fusion.2 = bf16[512,384]{1,0:T(8,128)(2,1)} fusion(bf16[768,384]{1,0:T(8,128)(2,1)} %reshape_reshape_reshape.10, s32[1024]{0:T(1024)S(1)} %pad_clamp_fusion), kind=kCustom, calls=%fused_computation.2 | custom fusion | bytes 788480 | tf_op jit(solution)/shard_map/gather | solution.py:108
  75.5 3.6 %fusion.36 = f32[512,4352]{1,0:T(8,128)S(1)} fusion(bf16[512,384]{1,0:T(8,128)(2,1)} %gather_fusion.2, bf16[384,4352]{1,0:T(8,128)(2,1)S(1)} %copy-done), kind=kOutput, calls=%fused_computation.75 | convolution fusion | flops 1711276032 | bytes 12648448 | tf_op jit(solution)/shard_map/dot_general | solution.py:112
  79.2 9.2 %fusion.35 = (bf16[512,4352]{1,0:T(8,128)(2,1)}, f32[512,4352]{1,0:T(8,128)S(1)}) fusion(f32[512,4352]{1,0:T(8,128)S(1)} %fusion.36, f32[8,4352]{1,0:T(8,128)S(1)} %copy-done.3, f32[4,128,8]{1,2,0:T(8,128)S(1)} %copy-done.4, pred[512]{0:T(512)(128)(4,1)S(1)} %fusion.30), kind=kOutput, calls=%fused_computation.74 | convolution fusion | flops 220594176 | bytes 22438400 | tf_op jit(solution)/shard_map/dot_general | solution.py:113
  88.4 3.4 %copy-done.1 = f32[512,4352]{1,0:T(8,128)} copy-done((f32[512,4352]{1,0:T(8,128)}, f32[512,4352]{1,0:T(8,128)S(1)}, u32[]{:S(2)}) %copy-start.1) | copy-done | bytes 8912920
  91.8 3.4 %fusion.4 = f32[512,384]{1,0:T(8,128)} fusion(bf16[384,4352]{1,0:T(8,128)(2,1)S(1)} %copy-done, f32[512,4352]{1,0:T(8,128)S(1)} %get-tuple-element.6, bf16[512,4352]{1,0:T(8,128)(2,1)S(1)} %bitcast.97, f32[4352]{0:T(1024)S(1)} %copy-done.5, pred[512]{0:T(512)(128)(4,1)S(1)} %fusion.30), kind=kOutput, calls=%fused_computation.12 | convolution fusion | flops 1722417152 | bytes 17516032 | tf_op jit(solution)/shard_map/dot_general | solution.py:118
  95.2 3.9 %scatter_custom_fusion.1 = f32[768,384]{1,0:T(8,128)} fusion(s32[512]{0:T(512)S(1)} %bitcast.110, f32[512,384]{1,0:T(8,128)} %fusion.4, f32[]{:T(128)} %constant.50.clone.1), kind=kCustom, calls=%fused_computation.25 | custom fusion | bytes 1180160 | tf_op jit(solution)/shard_map/scatter | solution.py:124
  99.1 3.3 %reshape_transpose_transpose_reshape_reshape_reshape_reshape.9 = f32[128,1,1,6,384]{4,2,3,1,0:T(1,128)} reshape(f32[768,384]{1,0:T(8,128)} %scatter_custom_fusion.1) | data formatting | bytes 2359296 | tf_op jit(solution)/shard_map/reshape;transpose;transpose;reshape;reshape;reshape;reshape | solution.py:29
  102.4 5.7 %all-to-all-start.2 = ((f32[128,1,1,6,384]{4,2,3,1,0:T(1,128)}), f32[128,1,1,6,384]{4,2,3,1,0:T(1,128)}, u32[]{:S(2)}, u32[]{:S(2)}) async-start(f32[128,1,1,6,384]{4,2,3,1,0:T(1,128)} %reshape_transpose_transpose_reshape_reshape_reshape_reshape.9), calls=%async_computation.2 | async-start | bytes 2359296 | tf_op jit(solution)/shard_map/all_to_all | solution.py:30
  108.1 0.0 reduce-scatter.4.cloned.1.call-start
  108.2 9.0 %convolution_multiply_fusion = f32[4352,8]{0,1:T(8,128)S(1)} fusion(f32[512,4352]{1,0:T(8,128)} %copy-done.1, bf16[512,4352]{1,0:T(8,128)(2,1)} %bitcast.94, f32[4352]{0:T(1024)S(1)} %copy-done.5, pred[512]{0:T(512)(128)(4,1)S(1)} %fusion.30, f32[4,128,8]{1,2,0:T(8,128)S(1)} %copy-done.4), kind=kOutput, calls=%fused_computation.10 | convolution fusion | flops 222857216 | bytes 13542912 | tf_op jit(solution)/shard_map/dot_general | solution.py:130
  117.2 1.5 reshape_reshape.3
  118.7 2.1 copy.23
  120.8 0.0 reduce-scatter.4.cloned.1.call-update
  120.8 0.0 reduce-scatter.6.cloned.1.call-start
  120.9 11.6 %reduce-scatter.4.cloned.1.call-done = f32[64,34,8]{1,2,0:T(8,128)} async-done(((f32[128,34,8]{1,2,0:T(8,128)}), f32[64,34,8]{1,2,0:T(8,128)}) %reduce-scatter.4.cloned.1.call-update) | async-done | bytes 69648 | tf_op jit(solution)/shard_map/reduce_scatter | solution.py:41
  132.4 0.0 reduce-scatter.6.cloned.1.call-update
  132.4 0.0 reduce-scatter.8.cloned.1.call-start
  132.5 24.9 %reduce-scatter.6.cloned.1.call-done = f32[16,34,8]{1,2,0:T(8,128)} async-done(((f32[64,34,8]{1,2,0:T(8,128)}), f32[16,34,8]{1,2,0:T(8,128)}) %reduce-scatter.6.cloned.1.call-update) | async-done | bytes 17424 | tf_op jit(solution)/shard_map/reduce_scatter | solution.py:41
  157.4 0.0 reduce-scatter.8.cloned.1.call-update
  157.5 0.6 dynamic-slice
  158.1 21.9 %reduce-scatter.8.cloned.1.call-done = f32[4,34,8]{1,2,0:T(8,128)} async-done(((f32[16,34,8]{1,2,0:T(8,128)}), f32[4,34,8]{1,2,0:T(8,128)}) %reduce-scatter.8.cloned.1.call-update) | async-done | bytes 4368 | tf_op jit(solution)/shard_map/reduce_scatter | solution.py:41
  179.9 17.5 %all-reduce = f32[4,34,8]{1,2,0:T(8,128)S(1)} all-reduce(f32[4,34,8]{1,2,0:T(8,128)} %reduce-scatter.8.cloned.1.call-done), channel_id=5, replica_groups=mesh['lat_0'=4,'lat_1'=2,'lon_0'=4,'lon_1'=4] {'lon_1'}, use_global_device_ids=true, to_apply=%region_9.10.clone | all-reduce | flops 1088 | bytes 8704
  197.4 1.2 dynamic-slice_bitcast_fusion
  198.7 2.6 %copy.25 = f32[8,16,1,1,6,384]{5,4,1,0,3,2:T(8,128)} copy(f32[8,16,1,1,6,384]{5,3,4,2,1,0:T(1,128)} %bitcast.21) | data formatting | bytes 2359296 | tf_op jit(solution)/shard_map/reshape | solution.py:31
  201.3 2.4 %reshape_reshape_reshape.11 = f32[768,384]{1,0:T(8,128)} reshape(f32[8,16,1,6,384]{4,3,1,0,2:T(8,128)} %bitcast.93) | data formatting | bytes 2359296 | tf_op jit(solution)/shard_map/reshape;reshape;reshape | solution.py:126
  203.8 8.7 %scatter_custom_fusion.2 = f32[1024,384]{1,0:T(8,128)} fusion(s32[768]{0:T(1024)S(1)} %fusion.25, f32[768,384]{1,0:T(8,128)} %reshape_reshape_reshape.11, bf16[768,384]{1,0:T(8,128)(2,1)} %gather_fusion.1, f32[]{:T(128)} %constant.50.clone.1, f32[]{:T(128)} %constant.49.clone.1, f32[]{:T(128)} %constant.48.clone.1), kind=kCustom, calls=%fused_computation.21 | custom fusion | flops 1474560 | bytes 3342348 | tf_op jit(solution)/shard_map/scatter-add | solution.py:127
  212.5 2.4 %convert_element_type.63 = bf16[1024,384]{1,0:T(8,128)(2,1)} convert(f32[1024,384]{1,0:T(8,128)} %scatter_custom_fusion.2) | non-fusion elementwise | flops 393216 | bytes 2359296 | tf_op jit(solution)/shard_map/convert_element_type | solution.py:128
  (28 shorter events, 0.2 us)
Async XLA Ops:
  7.2 68.3 %copy-start = (bf16[384,4352]{1,0:T(8,128)(2,1)S(1)}, bf16[384,4352]{1,0:T(8,128)(2,1)}, u32[]{:S(2)}) copy-start(bf16[384,4352]{1,0:T(8,128)(2,1)} %param.11) | copy-start | bytes 10027012
  9.2 0.7 copy-start.2
  43.8 10.3 %copy-start.6 = (s32[4]{0:T(128)S(1)}, s32[4]{0:T(128)}, u32[]{:S(2)}) copy-start(s32[4]{0:T(128)} %param.16) | copy-start | bytes 52
  48.2 21.6 %all-to-all-start.1 = ((bf16[128,1,1,6,384]{4,3,2,1,0:T(8,128)(2,1)}), bf16[128,1,1,6,384]{4,3,2,1,0:T(8,128)(2,1)}, u32[]{:S(2)}, u32[]{:S(2)}) async-start(bf16[128,1,1,6,384]{4,3,2,1,0:T(8,128)(2,1)} %bitcast.99), calls=%async_computation.1 | async-start | bytes 1572864 | tf_op jit(solution)/shard_map/all_to_all | solution.py:30
  75.5 3.6 %copy-start.3 = (f32[8,4352]{1,0:T(8,128)S(1)}, f32[8,4352]{1,0:T(8,128)}, u32[]{:S(2)}) copy-start(f32[8,4352]{1,0:T(8,128)} %param.14) | copy-start | bytes 417796
  75.5 3.7 %copy-start.4 = (f32[4,128,8]{1,2,0:T(8,128)S(1)}, f32[4,128,8]{1,2,0:T(8,128)}, u32[]{:S(2)}) copy-start(f32[4,128,8]{1,2,0:T(8,128)} %param.13) | copy-start | bytes 49156
  75.5 16.3 %slice-start = ((s8[4456448]{0:T(1024)(128)(4,1)}), s8[4194304]{0:T(1024)(128)(4,1)S(1)}, s32[]{:S(2)}) async-start(s8[4456448]{0:T(1024)(128)(4,1)} %bitcast.95), calls=%async_computation.9 | async-start | bytes 8388608
  79.2 12.6 %slice-start.1 = ((s8[4456448]{0:T(1024)(128)(4,1)}), s8[262144]{0:T(1024)(128)(4,1)S(1)}, s32[]{:S(2)}) async-start(s8[4456448]{0:T(1024)(128)(4,1)} %bitcast.95), calls=%async_computation.10 | async-start | bytes 524288
  79.2 12.6 %copy-start.5 = (f32[4352]{0:T(1024)S(1)}, f32[4352]{0:T(1024)}, u32[]{:S(2)}) copy-start(f32[4352]{0:T(1024)} %param.15) | copy-start | bytes 52228
  88.4 3.4 %copy-start.1 = (f32[512,4352]{1,0:T(8,128)}, f32[512,4352]{1,0:T(8,128)S(1)}, u32[]{:S(2)}) copy-start(f32[512,4352]{1,0:T(8,128)S(1)} %get-tuple-element.6) | copy-start | bytes 26738692
  102.4 96.3 %all-to-all-start.2 = ((f32[128,1,1,6,384]{4,2,3,1,0:T(1,128)}), f32[128,1,1,6,384]{4,2,3,1,0:T(1,128)}, u32[]{:S(2)}, u32[]{:S(2)}) async-start(f32[128,1,1,6,384]{4,2,3,1,0:T(1,128)} %reshape_transpose_transpose_reshape_reshape_reshape_reshape.9), calls=%async_computation.2 | async-start | bytes 2359296 | tf_op jit(solution)/shard_map/all_to_all | solution.py:30
  108.1 49.4 %copy-start.7 = (u32[128]{0:T(128)S(1)}, u32[128]{0:T(128)}, u32[]{:S(2)}) copy-start(u32[128]{0:T(128)} %constant.58) | copy-start | bytes 1540
  108.1 24.3 %reduce-scatter.4.cloned.1.call-start = ((), (), s32[]{:S(2)}) async-start(), calls=%async_computation.6 | async-start | bytes 786432 | tf_op jit(solution)/shard_map/reduce_scatter | solution.py:41
  120.8 36.6 %reduce-scatter.6.cloned.1.call-start = ((), (), s32[]{:S(2)}) async-start(), calls=%async_computation.7 | async-start | bytes 327680 | tf_op jit(solution)/shard_map/reduce_scatter | solution.py:41
  132.4 47.5 %reduce-scatter.8.cloned.1.call-start = ((), (), s32[]{:S(2)}) async-start(), calls=%async_computation.8 | async-start | bytes 81920 | tf_op jit(solution)/shard_map/reduce_scatter | solution.py:41
Sparse Core Ops, SparseCore 0:
  120.9 11.4 reduce-scatter.3
  134.8 22.6 reduce-scatter.5
  159.8 20.0 reduce-scatter.7
where the time goes:
time: 222 us; the launch traced here: 221 us
  waiting for transfers between devices  74.1 us (33%)
  local copies, waits for them, and re-layouts  41.1 us (19%)
  blocking collectives  38 us (17%)
  matrix products  25.2 us (11%)
  other arithmetic  17.4 us (8%)
  between operations  13.9 us (6%)
  starting transfers between devices  11.7 us (5%)
    reduce_scatter x3, waiting for transfers between devices, own_block(): parts = lax.psum_scatter(parts, axes[k], scatter_dimension=0, tiled=True)  58.4 us
    all_to_all x1, blocking collectives, one_exchange(): parts = lax.all_to_all(parts, axis, split_axis=0, concat_axis=0, tiled=True)  20.5 us
    unnamed x1, blocking collectives  17.5 us
    all_to_all x2, waiting for transfers between devices, one_exchange(): parts = lax.all_to_all(parts, axis, split_axis=0, concat_axis=0, tiled=True)  15.7 us
    all_to_all x2, starting transfers between devices, one_exchange(): parts = lax.all_to_all(parts, axis, split_axis=0, concat_axis=0, tiled=True)  11.6 us
    dot_general x1, matrix products, shards(): jnp.dot(flat_pred, beta_incr, precision=lax.Precision.HIGHEST)  9.19 us
    dot_general x1, matrix products, shards(): lax.dot_general(misfit, flat_pred, (((0,), (0,)), ((), ())), precision=la...  9.03 us
    scatter-add x1, other arithmetic, shards(): jnp.zeros((column_count, profile_len), jnp.float32).at[wanted].add(returned)  8.73 us
  transfers between devices with their start and end apart: 5, of which 4 were waited for; matrix products, arithmetic and copies ran while one was open for 7% of the time, Pallas kernels for 0%

commit v1 on v0

v1 whole, which is shorter than its diff:
```python
import jax
import jax.numpy as jnp
from jax import lax
from jax.experimental import pallas as pl
from jax.experimental.pallas import tpu as pltpu
from jax.sharding import Mesh
from jax.sharding import PartitionSpec as P

AXES = ("lat_0", "lat_1", "lon_0", "lon_1")
ROWS = 8
LANES = 128
PRED_STRIDE = 48
TILE = 256
F32 = jnp.float32
BF16 = jnp.bfloat16
VMEM = pl.BlockSpec(memory_space=pltpu.VMEM)
SMEM = pl.BlockSpec(memory_space=pltpu.SMEM)
ANY = pl.BlockSpec(memory_space=pl.ANY)


def iota(shape, dim):
    return lax.broadcasted_iota(jnp.int32, shape, dim)


def one_hot(mask):
    return jnp.where(mask, 1.0, 0.0).astype(BF16)


def dot(a, b, dims=((1,), (0,))):
    return lax.dot_general(a, b, (dims, ((), ())), preferred_element_type=F32)


def split(x):
    high = x.astype(BF16)
    return high, (x - high.astype(F32)).astype(BF16)


def index_kernel(count_ref, col_ref, req_ref, pos_ref, *, shift):
    blocks, block_len = col_ref.shape
    slots = blocks * block_len
    devices = req_ref.shape[0]
    cols = col_ref[...]
    owners = lax.shift_right_logical(cols, shift)
    local = (cols & ((1 << shift) - 1)) + 1
    owner_rows = iota((devices, block_len), 0)
    table = [one_hot(owner_rows == owners[k : k + 1, :]) for k in range(blocks)]
    table = jnp.concatenate(table, axis=1)
    earlier = one_hot(iota((slots, slots), 0) < iota((slots, slots), 1))
    counts = dot(table, earlier)
    ranked = jnp.sum(table.astype(F32) * counts, axis=0, keepdims=True).astype(jnp.int32)
    rank_rows = iota((LANES, block_len), 0)
    lane = iota((1, block_len), 1)
    high, low = [], []
    for k in range(blocks):
        rank = ranked[:, k * block_len : (k + 1) * block_len]
        mine = rank_rows == rank
        value = local[k : k + 1, :]
        high.append(jnp.where(mine, lax.shift_right_logical(value, 5), 0).astype(F32))
        low.append(jnp.where(mine, value & 31, 0).astype(F32))
        position = owners[k : k + 1, :] * ROWS + rank
        pos_ref[k : k + 1, :] = jnp.where(lane < count_ref[k], position, -1)
    high = jnp.concatenate(high, axis=1).astype(BF16)
    low = jnp.concatenate(low, axis=1).astype(BF16)
    nt = ((1,), (1,))
    req_ref[...] = (dot(table, high, nt) * 32.0 + dot(table, low, nt)).astype(jnp.int32) - 1


def owner_kernel(ids_ref, base_ref, step_ref, out_ref, pick_ref):
    devices = ids_ref.shape[0]
    columns = base_ref.shape[0]
    jacobian = 1.0 + 0.5 * jnp.tanh(base_ref[...].astype(F32))
    formed = (step_ref[...].astype(F32) * jacobian).astype(BF16)
    by_row = ids_ref[...].astype(F32).T[0:ROWS, :].astype(jnp.int32)
    lane = iota((2 * ROWS, columns), 1)
    for k in range(0, devices, 2):
        pair = [jnp.broadcast_to(by_row[:, d : d + 1], (ROWS, columns)) for d in (k, k + 1)]
        pair = jnp.concatenate(pair, axis=0)
        pick_ref[k * ROWS : (k + 2) * ROWS, :] = one_hot(pair == lane)
    out_ref[...] = dot(pick_ref[...], formed).astype(BF16)


def main_kernel(
    arrived_ref,
    pos_ref,
    pred_ref,
    beta_ref,
    weight_ref,
    count_ref,
    coef_hbm,
    dep_hbm,
    rad_hbm,
    out_ref,
    coef,
    dep,
    rad,
    mis,
    left,
    beta,
    sums,
    turned,
    coef_sem,
    dep_sem,
    rad_sem,
):
    blocks, npred, block_len = pred_ref.shape
    slots, channels = dep.shape
    profile = coef.shape[0]
    rows = arrived_ref.shape[0]
    devices = rows // ROWS
    share = channels // devices
    steps = channels // TILE

    def part(t):
        return pl.ds(t * TILE, TILE)

    def coef_copy(t):
        return pltpu.make_async_copy(coef_hbm.at[:, part(t)], coef.at[:, part(t)], coef_sem.at[t])

    def dep_copy(t):
        return pltpu.make_async_copy(dep_hbm.at[:, part(t)], dep.at[:, part(t)], dep_sem.at[t])

    def rad_copy(t):
        return pltpu.make_async_copy(rad.at[:, part(t)], rad_hbm.at[:, part(t)], rad_sem.at[t])

    for t in range(steps):
        coef_copy(t).start()
        dep_copy(t).start()

    lane = iota((1, block_len), 1)
    stack = []
    for k in range(blocks):
        here = pl.ds(k * block_len, block_len)
        row = jnp.broadcast_to(pos_ref[k : k + 1, :].astype(F32), (block_len, block_len))
        column = row.T.astype(jnp.int32)
        wide = jnp.concatenate([column] * (rows // block_len), axis=1)
        select = one_hot(wide == iota((block_len, rows), 1))
        left[here, 0:profile] = dot(select, arrived_ref[...]).astype(BF16)
        predictors = jnp.where(lane < count_ref[k], pred_ref[k], 0.0)
        high, low = split(predictors)
        high, low = high.astype(F32), low.astype(F32)
        stack.append(jnp.concatenate([high, low], axis=0))
        zeros = jnp.zeros((LANES - 4 * npred, block_len), F32)
        tall = jnp.concatenate([high, high, low, low, zeros], axis=0)
        left[here, profile : profile + LANES] = tall.T.astype(BF16)
    stack = jnp.concatenate(stack, axis=1).astype(BF16)
    high, low = split(beta_ref[...])
    high, low = high.astype(F32), low.astype(F32)
    zeros = jnp.zeros((LANES - 4 * npred, channels), F32)
    beta[...] = jnp.concatenate([high, low, high, low, zeros], axis=0).astype(BF16)

    for t in range(steps):
        cut = slice(t * TILE, (t + 1) * TILE)
        coef_copy(t).wait()
        right = jnp.concatenate([coef[:, cut], beta[:, cut]], axis=0)
        radiance = dot(left[...], right)
        rad[:, cut] = radiance.astype(BF16)
        rad_copy(t).start()
        dep_copy(t).wait()
        misfit = weight_ref[:, cut] * (radiance - dep[:, cut].astype(F32))
        high, low = split(misfit)
        mis[:, cut] = high
        from_high = dot(stack, high)
        from_low = dot(stack, low)
        sums[:, cut] = (
            from_high[0:npred] + from_high[npred:] + from_low[0:npred] + from_low[npred:]
        )

    pulled = dot(mis[...], coef[...], ((1,), (1,))).astype(BF16)

    for d in range(devices):
        turned[d, :, 0:share] = sums[:, d * share : (d + 1) * share]
    bias = jnp.concatenate(
        [
            jnp.concatenate(
                [turned[:, p, 0:share], jnp.zeros((devices, PRED_STRIDE - share), F32)], axis=1
            )
            for p in range(npred)
        ],
        axis=1,
    )
    high, low = split(bias)

    payload = jnp.concatenate([pulled, high, low], axis=0)
    step = 256
    for k in range(0, rows, step):
        index = iota((step, block_len), 0) + k
        place = [one_hot(index == pos_ref[b : b + 1, :]) for b in range(blocks)]
        device = iota((step, devices), 1) * ROWS
        index = iota((step, devices), 0) + k
        place += [one_hot(index == device + (ROWS - 2)), one_hot(index == device + (ROWS - 1))]
        place = jnp.concatenate(place, axis=1)
        out_ref[k : k + step, :] = dot(place, payload).astype(BF16)

    for t in range(steps):
        rad_copy(t).wait()


def final_kernel(ids_ref, base_ref, back_ref, grad_ref, bias_ref, *, scaling):
    devices = ids_ref.shape[0]
    columns = base_ref.shape[0]
    rows = back_ref.shape[0]
    npred, share = bias_ref.shape
    by_row = ids_ref[...].astype(F32).T[0:ROWS, :].astype(jnp.int32) + 1
    halves = jnp.concatenate(
        [lax.shift_right_logical(by_row, 5).astype(F32), (by_row & 31).astype(F32)], axis=0
    ).astype(BF16)
    spread = one_hot(lax.shift_right_logical(iota((devices, rows), 1), 3) == iota((devices, rows), 0))
    both = dot(halves, spread)
    both = both[0:ROWS] * 32.0 + both[ROWS:]
    mine = (iota((ROWS, rows), 1) & (ROWS - 1)) == iota((ROWS, rows), 0)
    wanted = jnp.sum(jnp.where(mine, both, 0.0), axis=0, keepdims=True).astype(jnp.int32) - 1
    step = 256
    for k in range(0, columns, step):
        place = one_hot(iota((step, rows), 0) + k == wanted)
        jacobian = 1.0 + 0.5 * jnp.tanh(base_ref[k : k + step, :].astype(F32))
        grad_ref[k : k + step, :] = (dot(place, back_ref[...]) * jacobian).astype(BF16)
    last = one_hot((iota((ROWS, rows), 1) & (ROWS - 1)) >= ROWS - 2)
    total = dot(last, back_ref[...])[0:1, :] * scaling
    for p in range(npred):
        bias_ref[p : p + 1, :] = total[:, p * PRED_STRIDE : p * PRED_STRIDE + share]


def exchange(x):
    return lax.all_to_all(x, AXES, split_axis=0, concat_axis=0, tiled=True)


def shards(
    background,
    increment,
    coefficients,
    departures,
    bias_pred,
    beta_incr,
    obs_weight,
    obs_count,
    col_index,
):
    devices = lax.axis_size(AXES)
    columns, profile = background.shape
    blocks, block_len = col_index.shape
    channels = coefficients.shape[1]
    npred = bias_pred.shape[2]
    slots = blocks * block_len
    rows = devices * ROWS
    shift = columns.bit_length() - 1
    assert columns == 1 << shift and channels % (TILE * 1) == 0
    scaling = float((slots * devices) ** -0.5)
    limit = pltpu.CompilerParams(vmem_limit_bytes=48 * 2**20)

    requests, position = pl.pallas_call(
        lambda *refs: index_kernel(*refs, shift=shift),
        out_shape=(
            jax.ShapeDtypeStruct((devices, LANES), jnp.int32),
            jax.ShapeDtypeStruct((blocks, block_len), jnp.int32),
        ),
        in_specs=[SMEM, VMEM],
        out_specs=(VMEM, VMEM),
        name="index",
    )(obs_count, col_index)
    ids = exchange(requests.reshape(devices, 1, LANES)).reshape(devices, LANES)

    formed = pl.pallas_call(
        owner_kernel,
        out_shape=jax.ShapeDtypeStruct((rows, profile), BF16),
        in_specs=[VMEM] * 3,
        out_specs=VMEM,
        scratch_shapes=[pltpu.VMEM((rows, columns), BF16)],
        name="owner",
    )(ids, background, increment)
    arrived = exchange(formed.reshape(devices, ROWS, profile)).reshape(rows, profile)

    steps = channels // TILE
    radiance, outgoing = pl.pallas_call(
        main_kernel,
        out_shape=(
            jax.ShapeDtypeStruct((slots, channels), BF16),
            jax.ShapeDtypeStruct((rows, profile), BF16),
        ),
        in_specs=[VMEM] * 5 + [SMEM] + [ANY] * 2,
        out_specs=(ANY, VMEM),
        scratch_shapes=[
            pltpu.VMEM((profile, channels), BF16),
            pltpu.VMEM((slots, channels), BF16),
            pltpu.VMEM((slots, channels), BF16),
            pltpu.VMEM((slots, channels), BF16),
            pltpu.VMEM((slots, profile + LANES), BF16),
            pltpu.VMEM((LANES, channels), BF16),
            pltpu.VMEM((npred, channels), F32),
            pltpu.VMEM((devices, npred, LANES), F32),
            pltpu.SemaphoreType.DMA((steps,)),
            pltpu.SemaphoreType.DMA((steps,)),
            pltpu.SemaphoreType.DMA((steps,)),
        ],
        compiler_params=limit,
        name="main",
    )(
        arrived,
        position,
        jnp.transpose(bias_pred, (0, 2, 1)),
        beta_incr,
        obs_weight.reshape(1, channels),
        obs_count,
        coefficients,
        departures.reshape(slots, channels),
    )
    returned = exchange(outgoing.reshape(devices, ROWS, profile)).reshape(rows, profile)

    column_grad, bias_grad = pl.pallas_call(
        lambda *refs: final_kernel(*refs, scaling=scaling),
        out_shape=(
            jax.ShapeDtypeStruct((columns, profile), BF16),
            jax.ShapeDtypeStruct((npred, channels // devices), F32),
        ),
        in_specs=[VMEM] * 3,
        out_specs=(VMEM, VMEM),
        name="final",
    )(ids, background, returned)
    return (
        radiance.reshape(blocks, block_len, channels),
        column_grad,
        jnp.transpose(bias_grad, (1, 0)),
    )


def solution(mesh):
    finer = Mesh(mesh.devices.reshape(4, 2, 4, 4), AXES)
    in_specs = (
        P(AXES, None),
        P(AXES, None),
        P(),
        P(AXES, None, None),
        P(AXES, None, None),
        P(),
        P(),
        P(AXES),
        P(AXES, None),
    )
    out_specs = (P(AXES, None, None), P(AXES, None), P(AXES, None))
    return jax.shard_map(
        shards, mesh=finer, in_specs=in_specs, out_specs=out_specs, check_vma=False
    )
```

time: 222 us -> 94.8 us (0.43)
  waiting for transfers between devices: 74.1 us -> 15 us
  local copies, waits for them, and re-layouts: 41.1 us -> 3.71 us
  Pallas kernels: 0 us -> 27.1 us
  matrix products: 25.2 us -> 0 us
  other arithmetic: 17.4 us -> 0 us
  between operations: 13.9 us -> 0.67 us
  starting transfers between devices: 11.7 us -> 5.86 us
  blocking collectives: 38 us -> 42 us
    reduce_scatter x3 -> x0, waiting for transfers between devices: 58.4 us -> none  [own_block(): parts = lax.psum_scatter(parts, axes[k], scatter_dimension=0, tiled=True)]
    pallas_call x0 -> x4, Pallas kernels: none -> 27.1 us  [the longest x1 17.7 us: shards(): pl.pallas_call(main_kernel, out_shape=(jax.ShapeDtypeStruct((slots, chann...]
    dot_general x4 -> x0, matrix products: 25.2 us -> none  [the longest x1 9.19 us: shards(): jnp.dot(flat_pred, beta_incr, precision=lax.Precision.HIGHEST)]
    all_to_all x1 -> x2, blocking collectives: 20.5 us -> 42 us  [exchange(): return lax.all_to_all(x, AXES, split_axis=0, concat_axis=0, tiled=True)]
    unnamed x1 -> x0, blocking collectives: 17.5 us -> none
    gather x3 -> x0, local copies, waits for them, and re-layouts: 12.3 us -> none  [the longest x1 4.34 us: shards(): step_rows = increment[wanted]]
    another operation x9 -> x0, local copies, waits for them, and re-layouts: 9.51 us -> none  [the longest x2 3.41 us: one_exchange(): parts = parts.reshape(-1, *inside)]
    scatter-add x1 -> x0, other arithmetic: 8.73 us -> none  [shards(): jnp.zeros((column_count, profile_len), jnp.float32).at[wanted].add(returned)]
  transfers between devices with their start and end apart: 5 -> 1, of which waited for: 4 -> 1; matrix products, arithmetic and copies ran while one was open for 7% -> 1% of each run, Pallas kernels for 0% -> 0%
where the time goes in v1:
time: 94.8 us; the launch traced here: 94.3 us
  blocking collectives  42 us (44%)
  Pallas kernels  27.1 us (29%)
  waiting for transfers between devices  15 us (16%)
  starting transfers between devices  5.86 us (6%)
  local copies, waits for them, and re-layouts  3.71 us (4%)
    all_to_all x2, blocking collectives, exchange(): return lax.all_to_all(x, AXES, split_axis=0, concat_axis=0, tiled=True)  42 us
    pallas_call x1, Pallas kernels, shards(): pl.pallas_call(main_kernel, out_shape=(jax.ShapeDtypeStruct((slots, chann...  17.7 us
    all_to_all x1, waiting for transfers between devices, exchange(): return lax.all_to_all(x, AXES, split_axis=0, concat_axis=0, tiled=True)  15 us
    all_to_all x1, starting transfers between devices, exchange(): return lax.all_to_all(x, AXES, split_axis=0, concat_axis=0, tiled=True)  5.86 us
    pallas_call x1, Pallas kernels, shards(): pl.pallas_call(lambda *refs: final_kernel(*refs, scaling=scaling), out_sh...  3.76 us
    pallas_call x1, Pallas kernels, shards(): pl.pallas_call(owner_kernel, out_shape=jax.ShapeDtypeStruct((rows, profil...  3.64 us
    unnamed x10, local copies, waits for them, and re-layouts  2.96 us
    pallas_call x1, Pallas kernels, shards(): pl.pallas_call(lambda *refs: index_kernel(*refs, shift=shift), out_shape=...  1.95 us
  transfers between devices with their start and end apart: 1, of which 1 were waited for; matrix products, arithmetic and copies ran while one was open for 1% of the time, Pallas kernels for 0%

profile of v1, /device:TPU:0, one launch (start us, length us, event | category | flops | bytes accessed | tf_op | source)
XLA Modules:
  0.0 94.3 jit_solution(16337343620153688019)
XLA Ops:
  0.6 0.0 copy-start
  0.6 2.0 %index.1 = (s32[128,128]{1,0:T(8,128)}, s32[4,128]{1,0:T(4,128)}) custom-call(s32[4]{0:T(128)} %count_ref.1, s32[4,128]{1,0:T(4,128)} %refs_1_.2), custom_call_target="tpu_custom_call" | custom-call | tf_op jit(solution)/shard_map/index/pallas_call | solution.py:250
  2.6 21.0 %all_to_all.15 = s32[128,1,128]{2,1,0:T(1,128)} all-to-all(s32[128,1,128]{2,1,0:T(1,128)} %bitcast.19), channel_id=1, replica_groups=mesh['lat_0'=4,'lat_1'=2,'lon_0'=4,'lon_1'=4] {'lat_0','lat_1','lon_0','..., dimensions={0} | all-to-all | bytes 131072 | tf_op jit(solution)/shard_map/all_to_all | solution.py:224
  23.6 3.6 %owner.1 = bf16[1024,384]{1,0:T(8,128)(2,1)} custom-call(s32[128,128]{1,0:T(8,128)} %bitcast.17, bf16[1024,384]{1,0:T(8,128)(2,1)} %refs_1_.3, bf16[1024,384]{1,0:T(8,128)(2,1)} %step_ref.1), custom_call_target="tpu_custom_call" | custom-call | tf_op jit(solution)/shard_map/owner/pallas_call | solution.py:262
  27.2 5.9 %all-to-all-start.1 = ((bf16[128,8,384]{2,1,0:T(8,128)(2,1)}), bf16[128,8,384]{2,1,0:T(8,128)(2,1)}, u32[]{:S(2)}, u32[]{:S(2)}) async-start(bf16[128,8,384]{2,1,0:T(8,128)(2,1)} %bitcast.16), calls=%async_computation.1 | async-start | bytes 1572864 | tf_op jit(solution)/shard_map/all_to_all | solution.py:224
  33.1 0.7 reshape.37.weight_ref
  33.8 15.0 %all-to-all-done.1 = bf16[128,8,384]{2,1,0:T(8,128)(2,1)} async-done(((bf16[128,8,384]{2,1,0:T(8,128)(2,1)}), bf16[128,8,384]{2,1,0:T(8,128)(2,1)}, u32[]{:S(2)}, u32[]{:S(2)}) %all-to-all-start.1) | async-done | bytes 786464 | tf_op jit(solution)/shard_map/all_to_all | solution.py:224
  48.9 0.0 copy-done
  48.9 0.0 copy-start.1
  48.9 0.9 copy-done.1
  49.8 0.0 copy-start.2
  49.8 0.7 copy-done.2
  50.5 0.0 copy-start.3
  50.5 0.7 copy-done.3
  51.2 0.0 copy-start.4
  51.2 0.7 copy-done.4
  51.8 17.7 %main.1 = (bf16[512,4352]{1,0:T(8,128)(2,1)}, bf16[1024,384]{1,0:T(8,128)(2,1)S(1)}) custom-call(bf16[1024,384]{1,0:T(8,128)(2,1)} %bitcast.4.arrived_ref, s32[4,128]{1,0:T(4,128)S(1)} %copy-done.3, f32[4,8,128]{2,1,0:T(8,128)S(1)} %bitcast.13, f32[8,4352]{1,0:T(8,128)S(1)} %copy-done.1, f32[1,4352]{1,0:T(1,128)S(1)} %reshape.37.weight_ref, s32[4]{0:T(128)S(1)} %copy-done.4, ...), custom_call_target="tpu_custom_call" | custom-call | tf_op jit(solution)/shard_map/main/pallas_call | solution.py:273
  69.6 21.0 %all_to_all.16 = bf16[128,8,384]{2,1,0:T(8,128)(2,1)} all-to-all(bf16[128,8,384]{2,1,0:T(8,128)(2,1)S(1)} %bitcast.12), channel_id=1, replica_groups=mesh['lat_0'=4,'lat_1'=2,'lon_0'=4,'lon_1'=4] {'lat_0','lat_1','lon_0','..., dimensions={0} | all-to-all | bytes 1572864 | tf_op jit(solution)/shard_map/all_to_all | solution.py:224
  90.5 3.8 %final.1 = (bf16[1024,384]{1,0:T(8,128)(2,1)}, f32[8,34]{1,0:T(8,128)}) custom-call(s32[128,128]{1,0:T(8,128)} %bitcast.18, bf16[1024,384]{1,0:T(8,128)(2,1)} %refs_1_.3, bf16[1024,384]{1,0:T(8,128)(2,1)} %bitcast.15), custom_call_target="tpu_custom_call" | custom-call | tf_op jit(solution)/shard_map/final/pallas_call | solution.py:308
Async XLA Ops:
  0.6 48.2 %copy-start = (bf16[384,4352]{1,0:T(8,128)(2,1)S(1)}, bf16[384,4352]{1,0:T(8,128)(2,1)}, u32[]{:S(2)}) copy-start(bf16[384,4352]{1,0:T(8,128)(2,1)} %coef_hbm.1) | copy-start | bytes 10027012
  27.2 21.6 %all-to-all-start.1 = ((bf16[128,8,384]{2,1,0:T(8,128)(2,1)}), bf16[128,8,384]{2,1,0:T(8,128)(2,1)}, u32[]{:S(2)}, u32[]{:S(2)}) async-start(bf16[128,8,384]{2,1,0:T(8,128)(2,1)} %bitcast.16), calls=%async_computation.1 | async-start | bytes 1572864 | tf_op jit(solution)/shard_map/all_to_all | solution.py:224
  48.9 0.9 copy-start.1
  49.8 0.7 copy-start.2
  50.5 0.7 copy-start.3
  51.2 0.7 copy-start.4

commit v2 on v1

v2 whole, which is shorter than its diff:
```python
import jax
import jax.numpy as jnp
from jax import lax
from jax.experimental import pallas as pl
from jax.experimental.pallas import tpu as pltpu
from jax.sharding import Mesh
from jax.sharding import PartitionSpec as P

AXES = ("lat_0", "lat_1", "lon_0", "lon_1")
ROWS = 8
LANES = 128
PRED_STRIDE = 48
TILE = 256
F32 = jnp.float32
BF16 = jnp.bfloat16
VMEM = pl.BlockSpec(memory_space=pltpu.VMEM)
SMEM = pl.BlockSpec(memory_space=pltpu.SMEM)
ANY = pl.BlockSpec(memory_space=pl.ANY)


def iota(shape, dim):
    return lax.broadcasted_iota(jnp.int32, shape, dim)


def one_hot(mask):
    return jnp.where(mask, 1.0, 0.0).astype(BF16)


def dot(a, b, dims=((1,), (0,))):
    return lax.dot_general(a, b, (dims, ((), ())), preferred_element_type=F32)


def split(x):
    high = x.astype(BF16)
    return high, (x - high.astype(F32)).astype(BF16)


def index_kernel(count_ref, col_ref, req_ref, pos_ref, *, shift):
    blocks, block_len = col_ref.shape
    slots = blocks * block_len
    devices = req_ref.shape[0]
    cols = col_ref[...]
    owners = lax.shift_right_logical(cols, shift)
    local = (cols & ((1 << shift) - 1)) + 1
    owner_rows = iota((devices, block_len), 0)
    table = [one_hot(owner_rows == owners[k : k + 1, :]) for k in range(blocks)]
    table = jnp.concatenate(table, axis=1)
    earlier = one_hot(iota((slots, slots), 0) < iota((slots, slots), 1))
    counts = dot(table, earlier)
    ranked = jnp.sum(table.astype(F32) * counts, axis=0, keepdims=True).astype(jnp.int32)
    rank_rows = iota((LANES, block_len), 0)
    lane = iota((1, block_len), 1)
    high, low = [], []
    for k in range(blocks):
        rank = ranked[:, k * block_len : (k + 1) * block_len]
        mine = rank_rows == rank
        value = local[k : k + 1, :]
        high.append(jnp.where(mine, lax.shift_right_logical(value, 5), 0).astype(F32))
        low.append(jnp.where(mine, value & 31, 0).astype(F32))
        position = owners[k : k + 1, :] * ROWS + rank
        pos_ref[k : k + 1, :] = jnp.where(lane < count_ref[k], position, -1)
    high = jnp.concatenate(high, axis=1).astype(BF16)
    low = jnp.concatenate(low, axis=1).astype(BF16)
    nt = ((1,), (1,))
    req_ref[...] = (dot(table, high, nt) * 32.0 + dot(table, low, nt)).astype(jnp.int32) - 1


def beta_rows(beta):
    high, low = split(beta)
    return jnp.concatenate([high.astype(F32), low.astype(F32)], axis=0).astype(BF16)


def form_kernel(base_ref, step_ref, form_ref):
    jacobian = 1.0 + 0.5 * jnp.tanh(base_ref[...].astype(F32))
    form_ref[...] = (step_ref[...].astype(F32) * jacobian).astype(BF16)


def second_kernel(
    pred_ref,
    count_ref,
    beta_ref,
    weight_ref,
    coef_hbm,
    dep_hbm,
    norm_ref,
    base_ref,
    sums_ref,
    side_ref,
    stack_ref,
    coef,
    dep,
    scaled,
    coef_sem,
    dep_sem,
):
    blocks, npred, block_len = pred_ref.shape
    profile, channels = coef.shape
    slots = dep.shape[0]
    pieces = coef_sem.shape[0]
    size = channels // pieces

    def coef_copy(t):
        cut = pl.ds(t * size, size)
        return pltpu.make_async_copy(coef_hbm.at[:, cut], coef.at[:, cut], coef_sem.at[t])

    def dep_copy(t):
        part = pl.ds(t * (slots // dep_sem.shape[0]), slots // dep_sem.shape[0])
        return pltpu.make_async_copy(dep_hbm.at[part], dep.at[part], dep_sem.at[t])

    for t in range(pieces):
        coef_copy(t).start()
    for t in range(dep_sem.shape[0]):
        dep_copy(t).start()

    lane = iota((1, block_len), 1)
    stack = []
    for k in range(blocks):
        predictors = jnp.where(lane < count_ref[k], pred_ref[k], 0.0)
        high, low = split(predictors)
        high, low = high.astype(F32), low.astype(F32)
        stack.append(jnp.concatenate([high, low], axis=0))
        zeros = jnp.zeros((LANES - 4 * npred, block_len), F32)
        tall = jnp.concatenate([high, high, low, low, zeros], axis=0)
        side_ref[k * block_len : (k + 1) * block_len, :] = tall.T.astype(BF16)
    stack = jnp.concatenate(stack, axis=1).astype(BF16)
    stack_ref[...] = stack
    for t in range(pieces):
        cut = slice(t * size, (t + 1) * size)
        coef_copy(t).wait()
        high, low = split(weight_ref[:, cut] * coef[:, cut].astype(F32))
        scaled[0:profile, cut] = high
        scaled[profile:, cut] = low
    for t in range(dep_sem.shape[0]):
        dep_copy(t).wait()
    nt = ((1,), (1,))
    pair = dot(dep[...], scaled[...], nt)
    base_ref[...] = pair[:, 0:profile] + pair[:, profile:]
    rows = jnp.concatenate([coef[...], beta_rows(beta_ref[...])], axis=0)
    pair = dot(rows, scaled[...], nt)
    high, low = split(pair[:, 0:profile] + pair[:, profile:])
    both = jnp.concatenate([high, low], axis=1)
    norm_ref[0 : profile + 2 * npred, :] = both
    norm_ref[profile + 2 * npred :, :] = both[profile:, :]
    sums = dot(stack, dep[...])
    sums_ref[...] = sums[0:npred] + sums[npred:]


def owner_kernel(ids_ref, form_ref, out_ref, pick_ref):
    devices = ids_ref.shape[0]
    columns = form_ref.shape[0]
    by_row = ids_ref[...].astype(F32).T[0:ROWS, :].astype(jnp.int32)
    lane = iota((2 * ROWS, columns), 1)
    for k in range(0, devices, 2):
        pair = [jnp.broadcast_to(by_row[:, d : d + 1], (ROWS, columns)) for d in (k, k + 1)]
        pair = jnp.concatenate(pair, axis=0)
        pick_ref[k * ROWS : (k + 2) * ROWS, :] = one_hot(pair == lane)
    out_ref[...] = dot(pick_ref[...], form_ref[...]).astype(BF16)


def main_kernel(
    arrived_ref,
    pos_ref,
    side_ref,
    stack_ref,
    norm_ref,
    base_ref,
    weight_ref,
    sums_ref,
    beta_ref,
    coef_hbm,
    out_ref,
    left_ref,
    sums,
    turned,
    coef,
    coef_sem,
):
    blocks, block_len = pos_ref.shape
    profile = arrived_ref.shape[1]
    rows = arrived_ref.shape[0]
    npred, channels = sums.shape
    devices = rows // ROWS
    share = channels // devices
    depth = norm_ref.shape[0]
    coef_copy = pltpu.make_async_copy(coef_hbm, coef, coef_sem)
    coef_copy.start()

    for k in range(blocks):
        here = pl.ds(k * block_len, block_len)
        row = jnp.broadcast_to(pos_ref[k : k + 1, :].astype(F32), (block_len, block_len))
        column = row.T.astype(jnp.int32)
        wide = jnp.concatenate([column] * (rows // block_len), axis=1)
        select = one_hot(wide == iota((block_len, rows), 1))
        left_ref[here, 0:profile] = dot(select, arrived_ref[...]).astype(BF16)
    left_ref[:, profile:] = side_ref[...]
    left = left_ref[:, 0:depth]

    pulled = dot(left, norm_ref[...])
    pulled = (pulled[:, 0:profile] + pulled[:, profile:] - base_ref[...]).astype(BF16)

    mixed = dot(stack_ref[...], left)
    high, low = split(mixed[0:npred] + mixed[npred:])
    mixed = jnp.concatenate([high.astype(F32), low.astype(F32)], axis=0).astype(BF16)
    tail = beta_rows(beta_ref[...])
    coef_copy.wait()
    mixed = dot(mixed, jnp.concatenate([coef[...], tail, tail], axis=0))
    sums[...] = weight_ref[...] * (mixed[0:npred] + mixed[npred:] - sums_ref[...])
    for d in range(devices):
        turned[d, :, 0:share] = sums[:, d * share : (d + 1) * share]
    bias = jnp.concatenate(
        [
            jnp.concatenate(
                [turned[:, p, 0:share], jnp.zeros((devices, PRED_STRIDE - share), F32)], axis=1
            )
            for p in range(npred)
        ],
        axis=1,
    )
    high, low = split(bias)
    payload = jnp.concatenate([pulled, high, low], axis=0)
    step = 256
    for k in range(0, rows, step):
        index = iota((step, block_len), 0) + k
        place = [one_hot(index == pos_ref[b : b + 1, :]) for b in range(blocks)]
        device = iota((step, devices), 1) * ROWS
        index = iota((step, devices), 0) + k
        place += [one_hot(index == device + (ROWS - 2)), one_hot(index == device + (ROWS - 1))]
        place = jnp.concatenate(place, axis=1)
        out_ref[k : k + step, :] = dot(place, payload).astype(BF16)


def radiance_kernel(left_ref, beta_ref, coef_hbm, out_hbm, out, coef, sem, coef_sem):
    profile, channels = coef.shape
    npred = beta_ref.shape[0]
    depth = profile + 4 * npred
    steps = channels // TILE

    def copy(t):
        cut = pl.ds(t * TILE, TILE)
        return pltpu.make_async_copy(out.at[:, cut], out_hbm.at[:, cut], sem.at[t])

    def coef_copy(t):
        cut = pl.ds(t * TILE, TILE)
        return pltpu.make_async_copy(coef_hbm.at[:, cut], coef.at[:, cut], coef_sem.at[t])

    for t in range(steps):
        coef_copy(t).start()
    tail = beta_rows(beta_ref[...])
    for t in range(steps):
        cut = slice(t * TILE, (t + 1) * TILE)
        coef_copy(t).wait()
        right = jnp.concatenate([coef[:, cut], tail[:, cut], tail[:, cut]], axis=0)
        out[:, cut] = dot(left_ref[:, 0:depth], right).astype(BF16)
        copy(t).start()
    for t in range(steps):
        copy(t).wait()


def final_kernel(ids_ref, base_ref, back_ref, grad_ref, bias_ref, *, scaling):
    devices = ids_ref.shape[0]
    columns = base_ref.shape[0]
    rows = back_ref.shape[0]
    npred, share = bias_ref.shape
    by_row = ids_ref[...].astype(F32).T[0:ROWS, :].astype(jnp.int32) + 1
    halves = jnp.concatenate(
        [lax.shift_right_logical(by_row, 5).astype(F32), (by_row & 31).astype(F32)], axis=0
    ).astype(BF16)
    spread = one_hot(lax.shift_right_logical(iota((devices, rows), 1), 3) == iota((devices, rows), 0))
    both = dot(halves, spread)
    both = both[0:ROWS] * 32.0 + both[ROWS:]
    mine = (iota((ROWS, rows), 1) & (ROWS - 1)) == iota((ROWS, rows), 0)
    wanted = jnp.sum(jnp.where(mine, both, 0.0), axis=0, keepdims=True).astype(jnp.int32) - 1
    step = 256
    for k in range(0, columns, step):
        place = one_hot(iota((step, rows), 0) + k == wanted)
        jacobian = 1.0 + 0.5 * jnp.tanh(base_ref[k : k + step, :].astype(F32))
        grad_ref[k : k + step, :] = (dot(place, back_ref[...]) * jacobian).astype(BF16)
    last = one_hot((iota((ROWS, rows), 1) & (ROWS - 1)) >= ROWS - 2)
    total = dot(last, back_ref[...])[0:1, :] * scaling
    for p in range(npred):
        bias_ref[p : p + 1, :] = total[:, p * PRED_STRIDE : p * PRED_STRIDE + share]


def exchange(x):
    return lax.all_to_all(x, AXES, split_axis=0, concat_axis=0, tiled=True)


def shards(
    background,
    increment,
    coefficients,
    departures,
    bias_pred,
    beta_incr,
    obs_weight,
    obs_count,
    col_index,
):
    devices = lax.axis_size(AXES)
    columns, profile = background.shape
    blocks, block_len = col_index.shape
    channels = coefficients.shape[1]
    npred = bias_pred.shape[2]
    slots = blocks * block_len
    rows = devices * ROWS
    shift = columns.bit_length() - 1
    assert columns == 1 << shift and channels % (TILE * 1) == 0
    scaling = float((slots * devices) ** -0.5)
    depth = profile + 4 * npred

    def shape(*dims, dtype=BF16):
        return jax.ShapeDtypeStruct(dims, dtype)

    def call(kernel, outs, inputs, flops, in_specs=None, out_specs=None, scratch=(), vmem=None):
        return pl.pallas_call(
            kernel,
            out_shape=outs,
            in_specs=in_specs or [VMEM] * len(inputs),
            out_specs=out_specs or jax.tree.map(lambda _: VMEM, outs),
            scratch_shapes=scratch,
            compiler_params=pltpu.CompilerParams(vmem_limit_bytes=vmem and vmem * 2**20),
            cost_estimate=pl.CostEstimate(
                flops=int(flops), bytes_accessed=4 * 2**20, transcendentals=0
            ),
        )(*inputs)

    flat_dep = pltpu.with_memory_space_constraint(departures.reshape(slots, channels), pltpu.HBM)
    coef_hbm = pltpu.with_memory_space_constraint(coefficients, pltpu.HBM)
    weight = obs_weight.reshape(1, channels)
    requests, position = call(
        lambda *refs: index_kernel(*refs, shift=shift),
        (shape(devices, LANES, dtype=jnp.int32), shape(blocks, block_len, dtype=jnp.int32)),
        (obs_count, col_index),
        1e8,
        in_specs=[SMEM, VMEM],
    )
    ids = exchange(requests.reshape(devices, 1, LANES)).reshape(devices, LANES)
    formed = call(form_kernel, shape(columns, profile), (background, increment), 3e9, vmem=16)
    rows_out = call(
        owner_kernel,
        shape(rows, profile),
        (ids, formed),
        1e9,
        scratch=[pltpu.VMEM((rows, columns), BF16)],
        vmem=16,
    )
    arrived = exchange(rows_out.reshape(devices, ROWS, profile)).reshape(rows, profile)
    norm, base, base_sums, side, stack = call(
        second_kernel,
        (
            shape(depth, 2 * profile),
            shape(slots, profile, dtype=F32),
            shape(npred, channels, dtype=F32),
            shape(slots, LANES),
            shape(2 * npred, slots),
        ),
        (jnp.transpose(bias_pred, (0, 2, 1)), obs_count, beta_incr, weight, coef_hbm, flat_dep),
        8e9,
        in_specs=[VMEM, SMEM, VMEM, VMEM, ANY, ANY],
        scratch=[
            pltpu.VMEM((profile, channels), BF16),
            pltpu.VMEM((slots, channels), BF16),
            pltpu.VMEM((2 * profile, channels), BF16),
            pltpu.SemaphoreType.DMA((channels // TILE,)),
            pltpu.SemaphoreType.DMA((4,)),
        ],
        vmem=32,
    )
    outgoing, left = call(
        main_kernel,
        (shape(rows, profile), shape(slots, profile + LANES)),
        (arrived, position, side, stack, norm, base, weight, base_sums, beta_incr, coef_hbm),
        2e9,
        in_specs=[VMEM] * 9 + [ANY],
        scratch=[
            pltpu.VMEM((npred, channels), F32),
            pltpu.VMEM((devices, npred, LANES), F32),
            pltpu.VMEM((profile, channels), BF16),
            pltpu.SemaphoreType.DMA,
        ],
        vmem=24,
    )
    returned = exchange(outgoing.reshape(devices, ROWS, profile)).reshape(rows, profile)
    radiance = call(
        radiance_kernel,
        shape(slots, channels),
        (left, beta_incr, coef_hbm),
        3e9,
        in_specs=[VMEM, VMEM, ANY],
        out_specs=ANY,
        scratch=[
            pltpu.VMEM((slots, channels), BF16),
            pltpu.VMEM((profile, channels), BF16),
            pltpu.SemaphoreType.DMA((channels // TILE,)),
            pltpu.SemaphoreType.DMA((channels // TILE,)),
        ],
        vmem=32,
    )
    column_grad, bias_grad = call(
        lambda *refs: final_kernel(*refs, scaling=scaling),
        (shape(columns, profile), shape(npred, channels // devices, dtype=F32)),
        (ids, background, returned),
        1e9,
        vmem=16,
    )
    return (
        radiance.reshape(blocks, block_len, channels),
        column_grad,
        jnp.transpose(bias_grad, (1, 0)),
    )


def solution(mesh):
    finer = Mesh(mesh.devices.reshape(4, 2, 4, 4), AXES)
    in_specs = (
        P(AXES, None),
        P(AXES, None),
        P(),
        P(AXES, None, None),
        P(AXES, None, None),
        P(),
        P(),
        P(AXES),
        P(AXES, None),
    )
    out_specs = (P(AXES, None, None), P(AXES, None), P(AXES, None))
    return jax.shard_map(
        shards, mesh=finer, in_specs=in_specs, out_specs=out_specs, check_vma=False
    )
```

time: 94.8 us -> 75.4 us (0.80)
  blocking collectives: 42 us -> 0 us
  starting transfers between devices: 5.86 us -> 20.8 us
  Pallas kernels: 27.1 us -> 32.3 us
  waiting for transfers between devices: 15 us -> 18.8 us
  local copies, waits for them, and re-layouts: 3.71 us -> 2.31 us
    all_to_all x2 -> x0, blocking collectives: 42 us -> none  [exchange(): return lax.all_to_all(x, AXES, split_axis=0, concat_axis=0, tiled=True)]
    all_to_all x1 -> x3, starting transfers between devices: 5.86 us -> 20.8 us  [exchange(): return lax.all_to_all(x, AXES, split_axis=0, concat_axis=0, tiled=True)]
    pallas_call x4 -> x7, Pallas kernels: 27.1 us -> 32.3 us  [call(): pl.pallas_call(kernel, out_shape=outs, in_specs=in_specs or [VMEM] * len(...]
    all_to_all x1 -> x3, waiting for transfers between devices: 15 us -> 18.8 us  [exchange(): return lax.all_to_all(x, AXES, split_axis=0, concat_axis=0, tiled=True)]
    unnamed x10 -> x16, local copies, waits for them, and re-layouts: 2.96 us -> 2.3 us
  transfers between devices with their start and end apart: 1 -> 3, of which waited for: 1 -> 3; matrix products, arithmetic and copies ran while one was open for 1% -> 0% of each run, Pallas kernels for 0% -> 27%
where the time goes in v2:
time: 75.4 us; the launch traced here: 75 us
  Pallas kernels  32.3 us (43%)
  starting transfers between devices  20.8 us (28%)
  waiting for transfers between devices  18.8 us (25%)
  local copies, waits for them, and re-layouts  2.31 us (3%)
  between operations  0.78 us (1%)
    pallas_call x7, Pallas kernels, call(): pl.pallas_call(kernel, out_shape=outs, in_specs=in_specs or [VMEM] * len(...  32.3 us
    all_to_all x3, starting transfers between devices, exchange(): return lax.all_to_all(x, AXES, split_axis=0, concat_axis=0, tiled=True)  20.8 us
    all_to_all x3, waiting for transfers between devices, exchange(): return lax.all_to_all(x, AXES, split_axis=0, concat_axis=0, tiled=True)  18.8 us
    unnamed x16, local copies, waits for them, and re-layouts  2.3 us
  transfers between devices with their start and end apart: 3, of which 3 were waited for; matrix products, arithmetic and copies ran while one was open for 0% of the time, Pallas kernels for 27%

profile of v2, /device:TPU:0, one launch (start us, length us, event | category | flops | bytes accessed | tf_op | source)
XLA Modules:
  0.0 75.0 jit_solution(3920469008732005970)
XLA Ops:
  0.6 1.8 %shard_map.112 = (s32[128,128]{1,0:T(8,128)}, s32[4,128]{1,0:T(4,128)}) custom-call(s32[4]{0:T(128)} %count_ref.1, s32[4,128]{1,0:T(4,128)} %refs_1_.2), custom_call_target="tpu_custom_call" | custom-call | flops 100000000 | bytes 4194304 | tf_op jit(solution)/shard_map/pallas_call | solution.py:315
  2.4 11.2 %all-to-all-start = ((s32[128,1,128]{2,1,0:T(1,128)}), s32[128,1,128]{2,1,0:T(1,128)S(1)}, u32[]{:S(2)}, u32[]{:S(2)}) async-start(s32[128,1,128]{2,1,0:T(1,128)} %bitcast.17), calls=%async_computation | async-start | bytes 131072 | tf_op jit(solution)/shard_map/all_to_all | solution.py:285
  13.6 0.0 copy-start
  13.6 1.1 %copy-done = bf16[1024,384]{1,0:T(8,128)(2,1)S(1)} copy-done((bf16[1024,384]{1,0:T(8,128)(2,1)S(1)}, bf16[1024,384]{1,0:T(8,128)(2,1)}, u32[]{:S(2)}) %copy-start) | copy-done | bytes 786456
  14.8 0.0 copy-start.1
  14.8 1.1 %copy-done.1 = bf16[1024,384]{1,0:T(8,128)(2,1)S(1)} copy-done((bf16[1024,384]{1,0:T(8,128)(2,1)S(1)}, bf16[1024,384]{1,0:T(8,128)(2,1)}, u32[]{:S(2)}) %copy-start.1) | copy-done | bytes 786456
  15.9 0.3 shard_map.113.form_ref
  16.2 0.0 copy-start.7
  16.2 0.0 copy-start.3
  16.3 0.0 copy-start.4
  16.3 0.0 copy-start.5
  16.3 6.8 %all-to-all-done = s32[128,1,128]{2,1,0:T(1,128)S(1)} async-done(((s32[128,1,128]{2,1,0:T(1,128)}), s32[128,1,128]{2,1,0:T(1,128)S(1)}, u32[]{:S(2)}, u32[]{:S(2)}) %all-to-all-start) | async-done | bytes 65568 | tf_op jit(solution)/shard_map/all_to_all | solution.py:285
  23.1 2.3 %shard_map.114 = bf16[1024,384]{1,0:T(8,128)(2,1)} custom-call(s32[128,128]{1,0:T(8,128)S(1)} %bitcast.14, bf16[1024,384]{1,0:T(8,128)(2,1)S(1)} %shard_map.113.form_ref), custom_call_target="tpu_custom_call" | custom-call | flops 1000000000 | bytes 4194304 | tf_op jit(solution)/shard_map/pallas_call | solution.py:315
  25.3 4.8 %all-to-all-start.1 = ((bf16[128,8,384]{2,1,0:T(8,128)(2,1)}), bf16[128,8,384]{2,1,0:T(8,128)(2,1)S(1)}, u32[]{:S(2)}, u32[]{:S(2)}) async-start(bf16[128,8,384]{2,1,0:T(8,128)(2,1)} %bitcast.3), calls=%async_computation.1 | async-start | bytes 1572864 | tf_op jit(solution)/shard_map/all_to_all | solution.py:285
  30.1 0.0 copy-done.7
  30.2 0.0 copy-done.3
  30.2 0.0 copy-done.4
  30.2 0.0 copy-done.5
  30.2 0.0 copy-start.6
  30.2 11.1 %shard_map.115 = (bf16[416,768]{1,0:T(8,128)(2,1)S(1)}, f32[512,384]{1,0:T(8,128)S(1)}, f32[8,4352]{1,0:T(8,128)S(1)}, bf16[512,128]{1,0:T(8,128)(2,1)S(1)}, bf16[16,512]{1,0:T(8,128)(2,1)S(1)}) custom-call(f32[4,8,128]{2,1,0:T(8,128)S(1)} %bitcast.16, s32[4]{0:T(128)S(1)} %copy-done.5, f32[8,4352]{1,0:T(8,128)S(1)} %copy-done.3, ...), custom_call_target="tpu_custom_call" | custom-call | flops 8000000000 | bytes 4194304 | tf_op jit(solution)/shard_map/pallas_call | solution.py:315
  41.3 5.0 %all-to-all-done.1 = bf16[128,8,384]{2,1,0:T(8,128)(2,1)S(1)} async-done(((bf16[128,8,384]{2,1,0:T(8,128)(2,1)}), bf16[128,8,384]{2,1,0:T(8,128)(2,1)S(1)}, u32[]{:S(2)}, u32[]{:S(2)}) %all-to-all-start.1) | async-done | bytes 786464 | tf_op jit(solution)/shard_map/all_to_all | solution.py:285
  46.2 0.0 copy-done.6
  46.3 5.4 %shard_map.116 = (bf16[1024,384]{1,0:T(8,128)(2,1)}, bf16[512,512]{1,0:T(8,128)(2,1)S(1)}) custom-call(bf16[1024,384]{1,0:T(8,128)(2,1)S(1)} %bitcast.12, s32[4,128]{1,0:T(4,128)S(1)} %copy-done.6, bf16[512,128]{1,0:T(8,128)(2,1)S(1)} %get-tuple-element.16.side_ref, bf16[16,512]{1,0:T(8,128)(2,1)S(1)} %get-tuple-element.17.stack_ref, ...), custom_call_target="tpu_custom_call" | custom-call | flops 2000000000 | bytes 4194304 | tf_op jit(solution)/shard_map/pallas_call | solution.py:315
  51.7 4.9 %all-to-all-start.2 = ((bf16[128,8,384]{2,1,0:T(8,128)(2,1)}), bf16[128,8,384]{2,1,0:T(8,128)(2,1)S(1)}, u32[]{:S(2)}, u32[]{:S(2)}) async-start(bf16[128,8,384]{2,1,0:T(8,128)(2,1)} %bitcast.8), calls=%async_computation.2 | async-start | bytes 1572864 | tf_op jit(solution)/shard_map/all_to_all | solution.py:285
  56.5 0.0 copy-start.2
  56.5 9.0 %shard_map.117 = bf16[512,4352]{1,0:T(8,128)(2,1)} custom-call(bf16[512,512]{1,0:T(8,128)(2,1)S(1)} %get-tuple-element.21.left_ref, f32[8,4352]{1,0:T(8,128)S(1)} %copy-done.3, bf16[384,4352]{1,0:T(8,128)(2,1)} %coef_hbm.5), custom_call_target="tpu_custom_call" | custom-call | flops 3000000000 | bytes 4194304 | tf_op jit(solution)/shard_map/pallas_call | solution.py:315
  65.6 7.0 %all-to-all-done.2 = bf16[128,8,384]{2,1,0:T(8,128)(2,1)S(1)} async-done(((bf16[128,8,384]{2,1,0:T(8,128)(2,1)}), bf16[128,8,384]{2,1,0:T(8,128)(2,1)S(1)}, u32[]{:S(2)}, u32[]{:S(2)}) %all-to-all-start.2) | async-done | bytes 786464 | tf_op jit(solution)/shard_map/all_to_all | solution.py:285
  72.6 0.0 copy-done.2
  72.6 2.4 %shard_map.118 = (bf16[1024,384]{1,0:T(8,128)(2,1)}, f32[8,34]{1,0:T(8,128)}) custom-call(s32[128,128]{1,0:T(8,128)S(1)} %bitcast.15, bf16[1024,384]{1,0:T(8,128)(2,1)S(1)} %copy-done.2, bf16[1024,384]{1,0:T(8,128)(2,1)S(1)} %bitcast.13), custom_call_target="tpu_custom_call" | custom-call | flops 1000000000 | bytes 4194304 | tf_op jit(solution)/shard_map/pallas_call | solution.py:315
  (1 shorter events, 0.0 us)
Async XLA Ops:
  2.4 20.6 %all-to-all-start = ((s32[128,1,128]{2,1,0:T(1,128)}), s32[128,1,128]{2,1,0:T(1,128)S(1)}, u32[]{:S(2)}, u32[]{:S(2)}) async-start(s32[128,1,128]{2,1,0:T(1,128)} %bitcast.17), calls=%async_computation | async-start | bytes 131072 | tf_op jit(solution)/shard_map/all_to_all | solution.py:285
  13.6 1.1 %copy-start = (bf16[1024,384]{1,0:T(8,128)(2,1)S(1)}, bf16[1024,384]{1,0:T(8,128)(2,1)}, u32[]{:S(2)}) copy-start(bf16[1024,384]{1,0:T(8,128)(2,1)} %step_ref.1) | copy-start | bytes 2359300
  14.8 1.1 %copy-start.1 = (bf16[1024,384]{1,0:T(8,128)(2,1)S(1)}, bf16[1024,384]{1,0:T(8,128)(2,1)}, u32[]{:S(2)}) copy-start(bf16[1024,384]{1,0:T(8,128)(2,1)} %refs_1_.3) | copy-start | bytes 2359300
  16.2 13.9 %copy-start.7 = (f32[4352]{0:T(1024)S(1)}, f32[4352]{0:T(1024)}, u32[]{:S(2)}) copy-start(f32[4352]{0:T(1024)} %param.15) | copy-start | bytes 52228
  16.2 13.9 %copy-start.3 = (f32[8,4352]{1,0:T(8,128)S(1)}, f32[8,4352]{1,0:T(8,128)}, u32[]{:S(2)}) copy-start(f32[8,4352]{1,0:T(8,128)} %beta_ref.5) | copy-start | bytes 417796
  16.3 13.9 %copy-start.4 = (f32[4,128,8]{1,2,0:T(8,128)S(1)}, f32[4,128,8]{1,2,0:T(8,128)}, u32[]{:S(2)}) copy-start(f32[4,128,8]{1,2,0:T(8,128)} %param.13) | copy-start | bytes 49156
  16.3 13.9 %copy-start.5 = (s32[4]{0:T(128)S(1)}, s32[4]{0:T(128)}, u32[]{:S(2)}) copy-start(s32[4]{0:T(128)} %count_ref.1) | copy-start | bytes 52
  25.3 20.9 %all-to-all-start.1 = ((bf16[128,8,384]{2,1,0:T(8,128)(2,1)}), bf16[128,8,384]{2,1,0:T(8,128)(2,1)S(1)}, u32[]{:S(2)}, u32[]{:S(2)}) async-start(bf16[128,8,384]{2,1,0:T(8,128)(2,1)} %bitcast.3), calls=%async_computation.1 | async-start | bytes 1572864 | tf_op jit(solution)/shard_map/all_to_all | solution.py:285
  30.2 16.1 %copy-start.6 = (s32[4,128]{1,0:T(4,128)S(1)}, s32[4,128]{1,0:T(4,128)}, u32[]{:S(2)}) copy-start(s32[4,128]{1,0:T(4,128)} %get-tuple-element.15.pos_ref) | copy-start | bytes 6148
  51.7 21.0 %all-to-all-start.2 = ((bf16[128,8,384]{2,1,0:T(8,128)(2,1)}), bf16[128,8,384]{2,1,0:T(8,128)(2,1)S(1)}, u32[]{:S(2)}, u32[]{:S(2)}) async-start(bf16[128,8,384]{2,1,0:T(8,128)(2,1)} %bitcast.8), calls=%async_computation.2 | async-start | bytes 1572864 | tf_op jit(solution)/shard_map/all_to_all | solution.py:285
  56.5 16.1 %copy-start.2 = (bf16[1024,384]{1,0:T(8,128)(2,1)S(1)}, bf16[1024,384]{1,0:T(8,128)(2,1)}, u32[]{:S(2)}) copy-start(bf16[1024,384]{1,0:T(8,128)(2,1)} %refs_1_.3) | copy-start | bytes 2359300

commit v3 on v2

--- a/solution.py
+++ b/solution.py
@@ -7,6 +7,7 @@
 from jax.sharding import PartitionSpec as P
 
 AXES = ("lat_0", "lat_1", "lon_0", "lon_1")
+RANKS = 6
 ROWS = 8
 LANES = 128
 PRED_STRIDE = 48
@@ -35,7 +36,18 @@
     return high, (x - high.astype(F32)).astype(BF16)
 
 
-def index_kernel(count_ref, col_ref, req_ref, pos_ref, *, shift):
+def index_kernel(
+    col_hbm, base_hbm, step_hbm, req_ref, pos_ref, form_ref, col_ref, base_ref, step_ref, sem, *, shift
+):
+    copies = [
+        pltpu.make_async_copy(source, target, sem.at[k])
+        for k, (source, target) in enumerate(
+            [(col_hbm, col_ref), (base_hbm, base_ref), (step_hbm, step_ref)]
+        )
+    ]
+    for copy in copies:
+        copy.start()
+    copies[0].wait()
     blocks, block_len = col_ref.shape
     slots = blocks * block_len
     devices = req_ref.shape[0]
@@ -49,7 +61,6 @@
     counts = dot(table, earlier)
     ranked = jnp.sum(table.astype(F32) * counts, axis=0, keepdims=True).astype(jnp.int32)
     rank_rows = iota((LANES, block_len), 0)
-    lane = iota((1, block_len), 1)
     high, low = [], []
     for k in range(blocks):
         rank = ranked[:, k * block_len : (k + 1) * block_len]
@@ -57,12 +68,15 @@
         value = local[k : k + 1, :]
         high.append(jnp.where(mine, lax.shift_right_logical(value, 5), 0).astype(F32))
         low.append(jnp.where(mine, value & 31, 0).astype(F32))
-        position = owners[k : k + 1, :] * ROWS + rank
-        pos_ref[k : k + 1, :] = jnp.where(lane < count_ref[k], position, -1)
+        pos_ref[k : k + 1, :] = owners[k : k + 1, :] * ROWS + rank
     high = jnp.concatenate(high, axis=1).astype(BF16)
     low = jnp.concatenate(low, axis=1).astype(BF16)
     nt = ((1,), (1,))
     req_ref[...] = (dot(table, high, nt) * 32.0 + dot(table, low, nt)).astype(jnp.int32) - 1
+    copies[1].wait()
+    copies[2].wait()
+    jacobian = 1.0 + 0.5 * jnp.tanh(base_ref[...].astype(F32))
+    form_ref[...] = (step_ref[...].astype(F32) * jacobian).astype(BF16)
 
 
 def beta_rows(beta):
@@ -70,18 +84,16 @@
     return jnp.concatenate([high.astype(F32), low.astype(F32)], axis=0).astype(BF16)
 
 
-def form_kernel(base_ref, step_ref, form_ref):
-    jacobian = 1.0 + 0.5 * jnp.tanh(base_ref[...].astype(F32))
-    form_ref[...] = (step_ref[...].astype(F32) * jacobian).astype(BF16)
-
-
 def second_kernel(
+    after_ref,
+    pos_ref,
     pred_ref,
     count_ref,
     beta_ref,
     weight_ref,
     coef_hbm,
     dep_hbm,
+    slot_ref,
     norm_ref,
     base_ref,
     sums_ref,
@@ -94,14 +106,14 @@
     dep_sem,
 ):
     blocks, npred, block_len = pred_ref.shape
-    profile, channels = coef.shape
+    profile, _ = coef.shape
     slots = dep.shape[0]
     pieces = coef_sem.shape[0]
-    size = channels // pieces
+    size = profile // pieces
 
     def coef_copy(t):
         cut = pl.ds(t * size, size)
-        return pltpu.make_async_copy(coef_hbm.at[:, cut], coef.at[:, cut], coef_sem.at[t])
+        return pltpu.make_async_copy(coef_hbm.at[cut], coef.at[cut], coef_sem.at[t])
 
     def dep_copy(t):
         part = pl.ds(t * (slots // dep_sem.shape[0]), slots // dep_sem.shape[0])
@@ -115,6 +127,7 @@
     lane = iota((1, block_len), 1)
     stack = []
     for k in range(blocks):
+        slot_ref[k : k + 1, :] = jnp.where(lane < count_ref[k], pos_ref[k : k + 1, :], -1)
         predictors = jnp.where(lane < count_ref[k], pred_ref[k], 0.0)
         high, low = split(predictors)
         high, low = high.astype(F32), low.astype(F32)
@@ -125,36 +138,39 @@
     stack = jnp.concatenate(stack, axis=1).astype(BF16)
     stack_ref[...] = stack
     for t in range(pieces):
+        coef_copy(t).wait()
         cut = slice(t * size, (t + 1) * size)
-        coef_copy(t).wait()
-        high, low = split(weight_ref[:, cut] * coef[:, cut].astype(F32))
-        scaled[0:profile, cut] = high
-        scaled[profile:, cut] = low
+        scaled[cut, :] = (weight_ref[...] * coef[cut, :].astype(F32)).astype(BF16)
+    nt = ((1,), (1,))
+    rows = jnp.concatenate([coef[...], beta_rows(beta_ref[...])], axis=0)
+    both = jnp.concatenate(split(dot(rows, scaled[...], nt)), axis=1)
+    norm_ref[0 : profile + 2 * npred, :] = both
+    norm_ref[profile + 2 * npred :, :] = both[profile:, :]
     for t in range(dep_sem.shape[0]):
         dep_copy(t).wait()
-    nt = ((1,), (1,))
-    pair = dot(dep[...], scaled[...], nt)
-    base_ref[...] = pair[:, 0:profile] + pair[:, profile:]
-    rows = jnp.concatenate([coef[...], beta_rows(beta_ref[...])], axis=0)
-    pair = dot(rows, scaled[...], nt)
-    high, low = split(pair[:, 0:profile] + pair[:, profile:])
-    both = jnp.concatenate([high, low], axis=1)
-    norm_ref[0 : profile + 2 * npred, :] = both
-    norm_ref[profile + 2 * npred :, :] = both[profile:, :]
+    base_ref[...] = dot(dep[...], scaled[...], nt)
     sums = dot(stack, dep[...])
     sums_ref[...] = sums[0:npred] + sums[npred:]
 
 
-def owner_kernel(ids_ref, form_ref, out_ref, pick_ref):
+def owner_kernel(ids_ref, form_ref, out_hbm, pick, wide, out, sem):
     devices = ids_ref.shape[0]
-    columns = form_ref.shape[0]
-    by_row = ids_ref[...].astype(F32).T[0:ROWS, :].astype(jnp.int32)
-    lane = iota((2 * ROWS, columns), 1)
-    for k in range(0, devices, 2):
-        pair = [jnp.broadcast_to(by_row[:, d : d + 1], (ROWS, columns)) for d in (k, k + 1)]
-        pair = jnp.concatenate(pair, axis=0)
-        pick_ref[k * ROWS : (k + 2) * ROWS, :] = one_hot(pair == lane)
-    out_ref[...] = dot(pick_ref[...], form_ref[...]).astype(BF16)
+    columns, profile = form_ref.shape
+    cuts = profile // LANES
+    group = RANKS * cuts
+    lane = iota((devices, columns), 1)
+    for r in range(RANKS):
+        pick[r * devices : (r + 1) * devices, :] = one_hot(ids_ref[:, r : r + 1] == lane)
+    result = dot(pick[...], form_ref[...])
+    for r in range(RANKS):
+        for c in range(cuts):
+            wide[pl.ds(c * RANKS + r, devices, stride=group), :] = result[
+                r * devices : (r + 1) * devices, c * LANES : (c + 1) * LANES
+            ]
+    out[...] = wide[...].astype(BF16)
+    copy = pltpu.make_async_copy(out, out_hbm, sem)
+    copy.start()
+    copy.wait()
 
 
 def main_kernel(
@@ -168,35 +184,62 @@
     sums_ref,
     beta_ref,
     coef_hbm,
-    out_ref,
+    out_hbm,
     left_ref,
     sums,
     turned,
+    placed,
     coef,
+    out,
+    table,
+    chosen,
     coef_sem,
+    out_sem,
 ):
     blocks, block_len = pos_ref.shape
-    profile = arrived_ref.shape[1]
-    rows = arrived_ref.shape[0]
+    rows, profile = out.shape
     npred, channels = sums.shape
     devices = rows // ROWS
+    cuts = profile // LANES
     share = channels // devices
     depth = norm_ref.shape[0]
     coef_copy = pltpu.make_async_copy(coef_hbm, coef, coef_sem)
     coef_copy.start()
 
+    count = devices * RANKS
+    group = RANKS * cuts
+    batch = 8
+    for g in range(devices // batch):
+        rows_in = arrived_ref[g * batch * group : (g + 1) * batch * group, :]
+        for c in range(cuts):
+            first = [d * group + c * RANKS for d in range(batch)]
+            part = jnp.concatenate([rows_in[f : f + RANKS, :] for f in first], axis=0)
+            here = slice(g * batch * RANKS, (g + 1) * batch * RANKS)
+            table[here, c * LANES : (c + 1) * LANES] = part
     for k in range(blocks):
         here = pl.ds(k * block_len, block_len)
-        row = jnp.broadcast_to(pos_ref[k : k + 1, :].astype(F32), (block_len, block_len))
-        column = row.T.astype(jnp.int32)
-        wide = jnp.concatenate([column] * (rows // block_len), axis=1)
-        select = one_hot(wide == iota((block_len, rows), 1))
-        left_ref[here, 0:profile] = dot(select, arrived_ref[...]).astype(BF16)
+        row = pos_ref[k : k + 1, :]
+        owner = lax.shift_right_arithmetic(row, ROWS.bit_length() - 1)
+        row = jnp.where(row < 0, -1, row - owner * (ROWS - RANKS))
+        column = jnp.broadcast_to(row.astype(F32), (block_len, block_len)).T.astype(jnp.int32)
+        lane = iota((block_len, count), 1)
+        chosen[here, :] = one_hot(jnp.concatenate([column] * (count // block_len), axis=1) == lane)
+    left_ref[:, 0:profile] = dot(chosen[...], table[...]).astype(BF16)
     left_ref[:, profile:] = side_ref[...]
     left = left_ref[:, 0:depth]
 
     pulled = dot(left, norm_ref[...])
     pulled = (pulled[:, 0:profile] + pulled[:, profile:] - base_ref[...]).astype(BF16)
+    step = rows // out_sem.shape[0]
+
+    def copy(t):
+        cut = pl.ds(t * step, step)
+        return pltpu.make_async_copy(out.at[cut], out_hbm.at[cut], out_sem.at[t])
+
+    for k in range(0, rows, step):
+        index = iota((step, block_len), 0) + k
+        place = [one_hot(index == pos_ref[b : b + 1, :]) for b in range(blocks)]
+        placed[k : k + step, :] = dot(jnp.concatenate(place, axis=1), pulled)
 
     mixed = dot(stack_ref[...], left)
     high, low = split(mixed[0:npred] + mixed[npred:])
@@ -216,17 +259,16 @@
         ],
         axis=1,
     )
-    high, low = split(bias)
-    payload = jnp.concatenate([pulled, high, low], axis=0)
-    step = 256
+    bias = jnp.concatenate(split(bias), axis=0)
     for k in range(0, rows, step):
-        index = iota((step, block_len), 0) + k
-        place = [one_hot(index == pos_ref[b : b + 1, :]) for b in range(blocks)]
         device = iota((step, devices), 1) * ROWS
         index = iota((step, devices), 0) + k
-        place += [one_hot(index == device + (ROWS - 2)), one_hot(index == device + (ROWS - 1))]
-        place = jnp.concatenate(place, axis=1)
-        out_ref[k : k + step, :] = dot(place, payload).astype(BF16)
+        place = [one_hot(index == device + (ROWS - 2)), one_hot(index == device + (ROWS - 1))]
+        extra = dot(jnp.concatenate(place, axis=1), bias)
+        out[k : k + step, :] = (placed[k : k + step, :] + extra).astype(BF16)
+        copy(k // step).start()
+    for k in range(rows // step):
+        copy(k).wait()
 
 
 def radiance_kernel(left_ref, beta_ref, coef_hbm, out_hbm, out, coef, sem, coef_sem):
@@ -239,16 +281,12 @@
         cut = pl.ds(t * TILE, TILE)
         return pltpu.make_async_copy(out.at[:, cut], out_hbm.at[:, cut], sem.at[t])
 
-    def coef_copy(t):
-        cut = pl.ds(t * TILE, TILE)
-        return pltpu.make_async_copy(coef_hbm.at[:, cut], coef.at[:, cut], coef_sem.at[t])
-
-    for t in range(steps):
-        coef_copy(t).start()
+    coef_copy = pltpu.make_async_copy(coef_hbm, coef, coef_sem)
+    coef_copy.start()
     tail = beta_rows(beta_ref[...])
+    coef_copy.wait()
     for t in range(steps):
         cut = slice(t * TILE, (t + 1) * TILE)
-        coef_copy(t).wait()
         right = jnp.concatenate([coef[:, cut], tail[:, cut], tail[:, cut]], axis=0)
         out[:, cut] = dot(left_ref[:, 0:depth], right).astype(BF16)
         copy(t).start()
@@ -307,6 +345,7 @@
     assert columns == 1 << shift and channels % (TILE * 1) == 0
     scaling = float((slots * devices) ** -0.5)
     depth = profile + 4 * npred
+    group = RANKS * profile // LANES
 
     def shape(*dims, dtype=BF16):
         return jax.ShapeDtypeStruct(dims, dtype)
@@ -316,7 +355,7 @@
             kernel,
             out_shape=outs,
             in_specs=in_specs or [VMEM] * len(inputs),
-            out_specs=out_specs or jax.tree.map(lambda _: VMEM, outs),
+            out_specs=out_specs or ([VMEM] * len(outs) if isinstance(outs, tuple) else VMEM),
             scratch_shapes=scratch,
             compiler_params=pltpu.CompilerParams(vmem_limit_bytes=vmem and vmem * 2**20),
             cost_estimate=pl.CostEstimate(
@@ -324,44 +363,75 @@
             ),
         )(*inputs)
 
-    flat_dep = pltpu.with_memory_space_constraint(departures.reshape(slots, channels), pltpu.HBM)
-    coef_hbm = pltpu.with_memory_space_constraint(coefficients, pltpu.HBM)
+    def in_hbm(x):
+        return pltpu.with_memory_space_constraint(x, pltpu.HBM)
+
+    flat_dep = in_hbm(departures.reshape(slots, channels))
+    coef_hbm = in_hbm(coefficients)
+    requests, position, formed = call(
+        lambda *refs: index_kernel(*refs, shift=shift),
+        (
+            shape(devices, LANES, dtype=jnp.int32),
+            shape(blocks, block_len, dtype=jnp.int32),
+            shape(columns, profile),
+        ),
+        (in_hbm(col_index), in_hbm(background), in_hbm(increment)),
+        1e8,
+        in_specs=[ANY] * 3,
+        scratch=[
+            pltpu.VMEM((blocks, block_len), jnp.int32),
+            pltpu.VMEM((columns, profile), BF16),
+            pltpu.VMEM((columns, profile), BF16),
+            pltpu.SemaphoreType.DMA((3,)),
+        ],
+        vmem=16,
+    )
+    ids = exchange(requests.reshape(devices, 1, LANES)).reshape(devices, LANES)
+    ids, obs_weight = lax.optimization_barrier((ids, obs_weight))
     weight = obs_weight.reshape(1, channels)
-    requests, position = call(
-        lambda *refs: index_kernel(*refs, shift=shift),
-        (shape(devices, LANES, dtype=jnp.int32), shape(blocks, block_len, dtype=jnp.int32)),
-        (obs_count, col_index),
-        1e8,
-        in_specs=[SMEM, VMEM],
-    )
-    ids = exchange(requests.reshape(devices, 1, LANES)).reshape(devices, LANES)
-    formed = call(form_kernel, shape(columns, profile), (background, increment), 3e9, vmem=16)
     rows_out = call(
         owner_kernel,
-        shape(rows, profile),
+        shape(devices * group, LANES),
         (ids, formed),
         1e9,
-        scratch=[pltpu.VMEM((rows, columns), BF16)],
+        out_specs=ANY,
+        scratch=[
+            pltpu.VMEM((devices * RANKS, columns), BF16),
+            pltpu.VMEM((devices * group, LANES), F32),
+            pltpu.VMEM((devices * group, LANES), BF16),
+            pltpu.SemaphoreType.DMA,
+        ],
         vmem=16,
     )
-    arrived = exchange(rows_out.reshape(devices, ROWS, profile)).reshape(rows, profile)
-    norm, base, base_sums, side, stack = call(
+    arrived = exchange(rows_out.reshape(devices, group // 2, 2, LANES))
+    arrived = arrived.reshape(devices * group, LANES)
+    slot_pos, norm, base, base_sums, side, stack = call(
         second_kernel,
         (
+            shape(blocks, block_len, dtype=jnp.int32),
             shape(depth, 2 * profile),
             shape(slots, profile, dtype=F32),
             shape(npred, channels, dtype=F32),
             shape(slots, LANES),
             shape(2 * npred, slots),
         ),
-        (jnp.transpose(bias_pred, (0, 2, 1)), obs_count, beta_incr, weight, coef_hbm, flat_dep),
+        (
+            ids,
+            position,
+            jnp.transpose(bias_pred, (0, 2, 1)),
+            obs_count,
+            beta_incr,
+            weight,
+            coef_hbm,
+            flat_dep,
+        ),
         8e9,
-        in_specs=[VMEM, SMEM, VMEM, VMEM, ANY, ANY],
+        in_specs=[ANY, VMEM, VMEM, SMEM, VMEM, VMEM, ANY, ANY],
         scratch=[
             pltpu.VMEM((profile, channels), BF16),
             pltpu.VMEM((slots, channels), BF16),
-            pltpu.VMEM((2 * profile, channels), BF16),
-            pltpu.SemaphoreType.DMA((channels // TILE,)),
+            pltpu.VMEM((profile, channels), BF16),
+            pltpu.SemaphoreType.DMA((4,)),
             pltpu.SemaphoreType.DMA((4,)),
         ],
         vmem=32,
@@ -369,14 +439,20 @@
     outgoing, left = call(
         main_kernel,
         (shape(rows, profile), shape(slots, profile + LANES)),
-        (arrived, position, side, stack, norm, base, weight, base_sums, beta_incr, coef_hbm),
+        (arrived, slot_pos, side, stack, norm, base, weight, base_sums, beta_incr, coef_hbm),
         2e9,
         in_specs=[VMEM] * 9 + [ANY],
+        out_specs=(ANY, VMEM),
         scratch=[
             pltpu.VMEM((npred, channels), F32),
             pltpu.VMEM((devices, npred, LANES), F32),
+            pltpu.VMEM((rows, profile), F32),
             pltpu.VMEM((profile, channels), BF16),
+            pltpu.VMEM((rows, profile), BF16),
+            pltpu.VMEM((devices * RANKS, profile), BF16),
+            pltpu.VMEM((slots, devices * RANKS), BF16),
             pltpu.SemaphoreType.DMA,
+            pltpu.SemaphoreType.DMA((4,)),
         ],
         vmem=24,
     )
@@ -392,7 +468,7 @@
             pltpu.VMEM((slots, channels), BF16),
             pltpu.VMEM((profile, channels), BF16),
             pltpu.SemaphoreType.DMA((channels // TILE,)),
-            pltpu.SemaphoreType.DMA((channels // TILE,)),
+            pltpu.SemaphoreType.DMA,
         ],
         vmem=32,
     )

time: 75.4 us -> 73.3 us (0.972)
  blocking collectives: 0 us -> 20.5 us
  starting transfers between devices: 20.8 us -> 9.46 us
  Pallas kernels: 32.3 us -> 26 us
  waiting for transfers between devices: 18.8 us -> 16.2 us
  local copies, waits for them, and re-layouts: 2.31 us -> 0.04 us
    all_to_all x0 -> x1, blocking collectives: none -> 20.5 us  [exchange(): return lax.all_to_all(x, AXES, split_axis=0, concat_axis=0, tiled=True)]
    all_to_all x3 -> x2, starting transfers between devices: 20.8 us -> 9.46 us  [exchange(): return lax.all_to_all(x, AXES, split_axis=0, concat_axis=0, tiled=True)]
    pallas_call x7 -> x6, Pallas kernels: 32.3 us -> 26 us  [call(): pl.pallas_call(kernel, out_shape=outs, in_specs=in_specs or [VMEM] * len(...]
    all_to_all x3 -> x2, waiting for transfers between devices: 18.8 us -> 16.2 us  [exchange(): return lax.all_to_all(x, AXES, split_axis=0, concat_axis=0, tiled=True)]
    unnamed x16 -> x10, local copies, waits for them, and re-layouts: 2.3 us -> 0.02 us
  transfers between devices with their start and end apart: 3 -> 2, of which waited for: 3 -> 2; matrix products, arithmetic and copies ran while one was open for 0% -> 0% of each run, Pallas kernels for 27% -> 19%
where the time goes in v3:
time: 73.3 us; the launch traced here: 73 us
  Pallas kernels  26 us (35%)
  blocking collectives  20.5 us (28%)
  waiting for transfers between devices  16.2 us (22%)
  starting transfers between devices  9.46 us (13%)
  between operations  0.77 us (1%)
    pallas_call x6, Pallas kernels, call(): pl.pallas_call(kernel, out_shape=outs, in_specs=in_specs or [VMEM] * len(...  26 us
    all_to_all x1, blocking collectives, exchange(): return lax.all_to_all(x, AXES, split_axis=0, concat_axis=0, tiled=True)  20.5 us
    all_to_all x2, waiting for transfers between devices, exchange(): return lax.all_to_all(x, AXES, split_axis=0, concat_axis=0, tiled=True)  16.2 us
    all_to_all x2, starting transfers between devices, exchange(): return lax.all_to_all(x, AXES, split_axis=0, concat_axis=0, tiled=True)  9.46 us
  transfers between devices with their start and end apart: 2, of which 2 were waited for; matrix products, arithmetic and copies ran while one was open for 0% of the time, Pallas kernels for 19%

profile of v3, /device:TPU:0, one launch (start us, length us, event | category | flops | bytes accessed | tf_op | source)
XLA Modules:
  0.0 73.0 jit_solution(13399523090285910264)
XLA Ops:
  0.6 0.0 copy-start.4
  0.6 0.0 copy-start.1
  0.7 0.0 copy-start.3
  0.7 0.0 copy-start.2
  0.7 1.8 %shard_map.112 = (s32[128,128]{1,0:T(8,128)S(1)}, s32[4,128]{1,0:T(4,128)S(1)}, bf16[1024,384]{1,0:T(8,128)(2,1)S(1)}) custom-call(s32[4,128]{1,0:T(4,128)} %refs_0_.1, bf16[1024,384]{1,0:T(8,128)(2,1)} %refs_1_.3, bf16[1024,384]{1,0:T(8,128)(2,1)} %refs_2_.1), custom_call_target="tpu_custom_call" | custom-call | flops 100000000 | bytes 4194304 | tf_op jit(solution)/shard_map/pallas_call | solution.py:354
  2.5 20.5 %all_to_all.15 = s32[128,1,128]{2,1,0:T(1,128)S(1)} all-to-all(s32[128,1,128]{2,1,0:T(1,128)S(1)} %bitcast.17), channel_id=1, replica_groups=mesh['lat_0'=4,'lat_1'=2,'lon_0'=4,'lon_1'=4] {'lat_0','lat_1','lon_0','..., dimensions={0} | all-to-all | bytes 131072 | tf_op jit(solution)/shard_map/all_to_all | solution.py:323
  23.0 1.9 %shard_map.113 = bf16[2304,128]{1,0:T(8,128)(2,1)} custom-call(s32[128,128]{1,0:T(8,128)S(1)} %bitcast.14, bf16[1024,384]{1,0:T(8,128)(2,1)S(1)} %get-tuple-element.20.form_ref), custom_call_target="tpu_custom_call" | custom-call | flops 1000000000 | bytes 4194304 | tf_op jit(solution)/shard_map/pallas_call | solution.py:354
  24.9 4.6 %all-to-all-start.1 = ((bf16[128,9,2,128]{3,2,1,0:T(2,128)(2,1)}), bf16[128,9,2,128]{3,2,1,0:T(2,128)(2,1)S(1)}, u32[]{:S(2)}, u32[]{:S(2)}) async-start(bf16[128,9,2,128]{3,2,1,0:T(2,128)(2,1)} %bitcast.3), calls=%async_computation.1 | async-start | bytes 1179648 | tf_op jit(solution)/shard_map/all_to_all | solution.py:323
  29.5 0.0 copy-done.4
  29.6 0.0 copy-done.1
  29.6 0.0 copy-done.3
  29.6 0.0 copy-done.2
  29.6 8.6 %shard_map.114 = (s32[4,128]{1,0:T(4,128)S(1)}, bf16[416,768]{1,0:T(8,128)(2,1)S(1)}, f32[512,384]{1,0:T(8,128)S(1)}, f32[8,4352]{1,0:T(8,128)S(1)}, bf16[512,12...) custom-call(s32[128,128]{1,0:T(8,128)S(1)} %bitcast.15, s32[4,128]{1,0:T(4,128)S(1)} %get-tuple-element.21.pos_ref, ...), custom_call_target="tpu_custom_call" | custom-call | flops 8000000000 | bytes 4194304 | tf_op jit(solution)/shard_map/pallas_call | solution.py:354
  38.2 5.6 %all-to-all-done.1 = bf16[128,9,2,128]{3,2,1,0:T(2,128)(2,1)S(1)} async-done(((bf16[128,9,2,128]{3,2,1,0:T(2,128)(2,1)}), bf16[128,9,2,128]{3,2,1,0:T(2,128)(2,1)S(1)}, u32[]{:S(2)}, u32[]{:S(2)}) %all-to-all-start.1) | async-done | bytes 589856 | tf_op jit(solution)/shard_map/all_to_all | solution.py:323
  43.8 5.9 %shard_map.115 = (bf16[1024,384]{1,0:T(8,128)(2,1)}, bf16[512,512]{1,0:T(8,128)(2,1)S(1)}) custom-call(bf16[2304,128]{1,0:T(8,128)(2,1)S(1)} %bitcast.13, s32[4,128]{1,0:T(4,128)S(1)} %get-tuple-element.23.pos_ref, bf16[512,128]{1,0:T(8,128)(2,1)S(1)} %get-tuple-element.24.side_ref, bf16[16,512]{1,0:T(8,128)(2,1)S(1)} %get-tuple-element.25.stack_ref, ...), custom_call_target="tpu_custom_call" | custom-call | flops 2000000000 | bytes 4194304 | tf_op jit(solution)/shard_map/pallas_call | solution.py:354
  49.7 4.8 %all-to-all-start.2 = ((bf16[128,8,384]{2,1,0:T(8,128)(2,1)}), bf16[128,8,384]{2,1,0:T(8,128)(2,1)S(1)}, u32[]{:S(2)}, u32[]{:S(2)}) async-start(bf16[128,8,384]{2,1,0:T(8,128)(2,1)} %bitcast.8), calls=%async_computation.2 | async-start | bytes 1572864 | tf_op jit(solution)/shard_map/all_to_all | solution.py:323
  54.5 0.0 copy-start
  54.5 5.5 %shard_map.116 = bf16[512,4352]{1,0:T(8,128)(2,1)} custom-call(bf16[512,512]{1,0:T(8,128)(2,1)S(1)} %get-tuple-element.29.left_ref, f32[8,4352]{1,0:T(8,128)S(1)} %copy-done.1, bf16[384,4352]{1,0:T(8,128)(2,1)} %coef_hbm.5), custom_call_target="tpu_custom_call" | custom-call | flops 3000000000 | bytes 4194304 | tf_op jit(solution)/shard_map/pallas_call | solution.py:354
  60.0 10.6 %all-to-all-done.2 = bf16[128,8,384]{2,1,0:T(8,128)(2,1)S(1)} async-done(((bf16[128,8,384]{2,1,0:T(8,128)(2,1)}), bf16[128,8,384]{2,1,0:T(8,128)(2,1)S(1)}, u32[]{:S(2)}, u32[]{:S(2)}) %all-to-all-start.2) | async-done | bytes 786464 | tf_op jit(solution)/shard_map/all_to_all | solution.py:323
  70.6 0.0 copy-done
  70.7 2.4 %shard_map.117 = (bf16[1024,384]{1,0:T(8,128)(2,1)}, f32[8,34]{1,0:T(8,128)}) custom-call(s32[128,128]{1,0:T(8,128)S(1)} %bitcast.16, bf16[1024,384]{1,0:T(8,128)(2,1)S(1)} %copy-done, bf16[1024,384]{1,0:T(8,128)(2,1)S(1)} %bitcast.12), custom_call_target="tpu_custom_call" | custom-call | flops 1000000000 | bytes 4194304 | tf_op jit(solution)/shard_map/pallas_call | solution.py:354
  (1 shorter events, 0.0 us)
Async XLA Ops:
  0.6 28.9 %copy-start.4 = (f32[4352]{0:T(1024)S(1)}, f32[4352]{0:T(1024)}, u32[]{:S(2)}) copy-start(f32[4352]{0:T(1024)} %param.15) | copy-start | bytes 52228
  0.6 28.9 %copy-start.1 = (f32[8,4352]{1,0:T(8,128)S(1)}, f32[8,4352]{1,0:T(8,128)}, u32[]{:S(2)}) copy-start(f32[8,4352]{1,0:T(8,128)} %beta_ref.5) | copy-start | bytes 417796
  0.7 28.9 %copy-start.3 = (s32[4]{0:T(128)S(1)}, s32[4]{0:T(128)}, u32[]{:S(2)}) copy-start(s32[4]{0:T(128)} %count_ref.1) | copy-start | bytes 52
  0.7 28.9 %copy-start.2 = (f32[4,128,8]{1,2,0:T(8,128)S(1)}, f32[4,128,8]{1,2,0:T(8,128)}, u32[]{:S(2)}) copy-start(f32[4,128,8]{1,2,0:T(8,128)} %param.13) | copy-start | bytes 49156
  24.9 18.9 %all-to-all-start.1 = ((bf16[128,9,2,128]{3,2,1,0:T(2,128)(2,1)}), bf16[128,9,2,128]{3,2,1,0:T(2,128)(2,1)S(1)}, u32[]{:S(2)}, u32[]{:S(2)}) async-start(bf16[128,9,2,128]{3,2,1,0:T(2,128)(2,1)} %bitcast.3), calls=%async_computation.1 | async-start | bytes 1179648 | tf_op jit(solution)/shard_map/all_to_all | solution.py:323
  49.7 21.0 %all-to-all-start.2 = ((bf16[128,8,384]{2,1,0:T(8,128)(2,1)}), bf16[128,8,384]{2,1,0:T(8,128)(2,1)S(1)}, u32[]{:S(2)}, u32[]{:S(2)}) async-start(bf16[128,8,384]{2,1,0:T(8,128)(2,1)} %bitcast.8), calls=%async_computation.2 | async-start | bytes 1572864 | tf_op jit(solution)/shard_map/all_to_all | solution.py:323
  54.5 16.1 %copy-start = (bf16[1024,384]{1,0:T(8,128)(2,1)S(1)}, bf16[1024,384]{1,0:T(8,128)(2,1)}, u32[]{:S(2)}) copy-start(bf16[1024,384]{1,0:T(8,128)(2,1)} %refs_1_.3) | copy-start | bytes 2359300

commit v4 on v3

--- a/solution.py
+++ b/solution.py
@@ -209,13 +209,20 @@
     count = devices * RANKS
     group = RANKS * cuts
     batch = 8
-    for g in range(devices // batch):
-        rows_in = arrived_ref[g * batch * group : (g + 1) * batch * group, :]
-        for c in range(cuts):
-            first = [d * group + c * RANKS for d in range(batch)]
-            part = jnp.concatenate([rows_in[f : f + RANKS, :] for f in first], axis=0)
-            here = slice(g * batch * RANKS, (g + 1) * batch * RANKS)
-            table[here, c * LANES : (c + 1) * LANES] = part
+
+    def reorder(half, carry):
+        for g in range(devices // batch // 2):
+            at = half * (devices // batch // 2) + g
+            start = pl.multiple_of(at * batch * group, 16)
+            rows_in = arrived_ref[pl.ds(start, batch * group), :]
+            here = pl.ds(pl.multiple_of(at * batch * RANKS, 16), batch * RANKS)
+            for c in range(cuts):
+                first = [d * group + c * RANKS for d in range(batch)]
+                part = jnp.concatenate([rows_in[f : f + RANKS, :] for f in first], axis=0)
+                table[here, c * LANES : (c + 1) * LANES] = part
+        return carry
+
+    lax.fori_loop(0, 2, reorder, 0)
     for k in range(blocks):
         here = pl.ds(k * block_len, block_len)
         row = pos_ref[k : k + 1, :]

time: 73.3 us -> 71.6 us (0.977)
  Pallas kernels: 26 us -> 24.3 us
    pallas_call x6, Pallas kernels: 26 us -> 24.3 us  [call(): pl.pallas_call(kernel, out_shape=outs, in_specs=in_specs or [VMEM] * len(...]
  transfers between devices with their start and end apart: 2 -> 2, of which waited for: 2 -> 2; matrix products, arithmetic and copies ran while one was open for 0% -> 0% of each run, Pallas kernels for 19% -> 20%
where the time goes in v4:
time: 71.6 us; the launch traced here: 71.3 us
  Pallas kernels  24.3 us (34%)
  blocking collectives  20.5 us (29%)
  waiting for transfers between devices  16.2 us (23%)
  starting transfers between devices  9.46 us (13%)
  between operations  0.77 us (1%)
    pallas_call x6, Pallas kernels, call(): pl.pallas_call(kernel, out_shape=outs, in_specs=in_specs or [VMEM] * len(...  24.3 us
    all_to_all x1, blocking collectives, exchange(): return lax.all_to_all(x, AXES, split_axis=0, concat_axis=0, tiled=True)  20.5 us
    all_to_all x2, waiting for transfers between devices, exchange(): return lax.all_to_all(x, AXES, split_axis=0, concat_axis=0, tiled=True)  16.2 us
    all_to_all x2, starting transfers between devices, exchange(): return lax.all_to_all(x, AXES, split_axis=0, concat_axis=0, tiled=True)  9.46 us
  transfers between devices with their start and end apart: 2, of which 2 were waited for; matrix products, arithmetic and copies ran while one was open for 0% of the time, Pallas kernels for 20%

profile of v4, /device:TPU:0, one launch (start us, length us, event | category | flops | bytes accessed | tf_op | source)
XLA Modules:
  0.0 71.3 jit_solution(823466296276009563)
XLA Ops:
  0.6 0.0 copy-start.4
  0.6 0.0 copy-start.1
  0.7 0.0 copy-start.3
  0.7 0.0 copy-start.2
  0.7 1.8 %shard_map.112 = (s32[128,128]{1,0:T(8,128)S(1)}, s32[4,128]{1,0:T(4,128)S(1)}, bf16[1024,384]{1,0:T(8,128)(2,1)S(1)}) custom-call(s32[4,128]{1,0:T(4,128)} %refs_0_.1, bf16[1024,384]{1,0:T(8,128)(2,1)} %refs_1_.3, bf16[1024,384]{1,0:T(8,128)(2,1)} %refs_2_.1), custom_call_target="tpu_custom_call" | custom-call | flops 100000000 | bytes 4194304 | tf_op jit(solution)/shard_map/pallas_call | solution.py:361
  2.5 20.5 %all_to_all.15 = s32[128,1,128]{2,1,0:T(1,128)S(1)} all-to-all(s32[128,1,128]{2,1,0:T(1,128)S(1)} %bitcast.17), channel_id=1, replica_groups=mesh['lat_0'=4,'lat_1'=2,'lon_0'=4,'lon_1'=4] {'lat_0','lat_1','lon_0','..., dimensions={0} | all-to-all | bytes 131072 | tf_op jit(solution)/shard_map/all_to_all | solution.py:330
  23.0 1.9 %shard_map.113 = bf16[2304,128]{1,0:T(8,128)(2,1)} custom-call(s32[128,128]{1,0:T(8,128)S(1)} %bitcast.14, bf16[1024,384]{1,0:T(8,128)(2,1)S(1)} %get-tuple-element.20.form_ref), custom_call_target="tpu_custom_call" | custom-call | flops 1000000000 | bytes 4194304 | tf_op jit(solution)/shard_map/pallas_call | solution.py:361
  24.9 4.6 %all-to-all-start.1 = ((bf16[128,9,2,128]{3,2,1,0:T(2,128)(2,1)}), bf16[128,9,2,128]{3,2,1,0:T(2,128)(2,1)S(1)}, u32[]{:S(2)}, u32[]{:S(2)}) async-start(bf16[128,9,2,128]{3,2,1,0:T(2,128)(2,1)} %bitcast.3), calls=%async_computation.1 | async-start | bytes 1179648 | tf_op jit(solution)/shard_map/all_to_all | solution.py:330
  29.5 0.0 copy-done.4
  29.6 0.0 copy-done.1
  29.6 0.0 copy-done.3
  29.6 0.0 copy-done.2
  29.6 8.6 %shard_map.114 = (s32[4,128]{1,0:T(4,128)S(1)}, bf16[416,768]{1,0:T(8,128)(2,1)S(1)}, f32[512,384]{1,0:T(8,128)S(1)}, f32[8,4352]{1,0:T(8,128)S(1)}, bf16[512,12...) custom-call(s32[128,128]{1,0:T(8,128)S(1)} %bitcast.15, s32[4,128]{1,0:T(4,128)S(1)} %get-tuple-element.21.pos_ref, ...), custom_call_target="tpu_custom_call" | custom-call | flops 8000000000 | bytes 4194304 | tf_op jit(solution)/shard_map/pallas_call | solution.py:361
  38.2 5.6 %all-to-all-done.1 = bf16[128,9,2,128]{3,2,1,0:T(2,128)(2,1)S(1)} async-done(((bf16[128,9,2,128]{3,2,1,0:T(2,128)(2,1)}), bf16[128,9,2,128]{3,2,1,0:T(2,128)(2,1)S(1)}, u32[]{:S(2)}, u32[]{:S(2)}) %all-to-all-start.1) | async-done | bytes 589856 | tf_op jit(solution)/shard_map/all_to_all | solution.py:330
  43.8 4.2 %shard_map.115 = (bf16[1024,384]{1,0:T(8,128)(2,1)}, bf16[512,512]{1,0:T(8,128)(2,1)S(1)}) custom-call(bf16[2304,128]{1,0:T(8,128)(2,1)S(1)} %bitcast.13, s32[4,128]{1,0:T(4,128)S(1)} %get-tuple-element.23.pos_ref, bf16[512,128]{1,0:T(8,128)(2,1)S(1)} %get-tuple-element.24.side_ref, bf16[16,512]{1,0:T(8,128)(2,1)S(1)} %get-tuple-element.25.stack_ref, ...), custom_call_target="tpu_custom_call" | custom-call | flops 2000000000 | bytes 4194304 | tf_op jit(solution)/shard_map/pallas_call | solution.py:361
  48.0 4.8 %all-to-all-start.2 = ((bf16[128,8,384]{2,1,0:T(8,128)(2,1)}), bf16[128,8,384]{2,1,0:T(8,128)(2,1)S(1)}, u32[]{:S(2)}, u32[]{:S(2)}) async-start(bf16[128,8,384]{2,1,0:T(8,128)(2,1)} %bitcast.8), calls=%async_computation.2 | async-start | bytes 1572864 | tf_op jit(solution)/shard_map/all_to_all | solution.py:330
  52.9 0.0 copy-start
  52.9 5.5 %shard_map.116 = bf16[512,4352]{1,0:T(8,128)(2,1)} custom-call(bf16[512,512]{1,0:T(8,128)(2,1)S(1)} %get-tuple-element.29.left_ref, f32[8,4352]{1,0:T(8,128)S(1)} %copy-done.1, bf16[384,4352]{1,0:T(8,128)(2,1)} %coef_hbm.5), custom_call_target="tpu_custom_call" | custom-call | flops 3000000000 | bytes 4194304 | tf_op jit(solution)/shard_map/pallas_call | solution.py:361
  58.4 10.6 %all-to-all-done.2 = bf16[128,8,384]{2,1,0:T(8,128)(2,1)S(1)} async-done(((bf16[128,8,384]{2,1,0:T(8,128)(2,1)}), bf16[128,8,384]{2,1,0:T(8,128)(2,1)S(1)}, u32[]{:S(2)}, u32[]{:S(2)}) %all-to-all-start.2) | async-done | bytes 786464 | tf_op jit(solution)/shard_map/all_to_all | solution.py:330
  69.0 0.0 copy-done
  69.0 2.4 %shard_map.117 = (bf16[1024,384]{1,0:T(8,128)(2,1)}, f32[8,34]{1,0:T(8,128)}) custom-call(s32[128,128]{1,0:T(8,128)S(1)} %bitcast.16, bf16[1024,384]{1,0:T(8,128)(2,1)S(1)} %copy-done, bf16[1024,384]{1,0:T(8,128)(2,1)S(1)} %bitcast.12), custom_call_target="tpu_custom_call" | custom-call | flops 1000000000 | bytes 4194304 | tf_op jit(solution)/shard_map/pallas_call | solution.py:361
  (1 shorter events, 0.0 us)
Async XLA Ops:
  0.6 28.9 %copy-start.4 = (f32[4352]{0:T(1024)S(1)}, f32[4352]{0:T(1024)}, u32[]{:S(2)}) copy-start(f32[4352]{0:T(1024)} %param.15) | copy-start | bytes 52228
  0.6 28.9 %copy-start.1 = (f32[8,4352]{1,0:T(8,128)S(1)}, f32[8,4352]{1,0:T(8,128)}, u32[]{:S(2)}) copy-start(f32[8,4352]{1,0:T(8,128)} %beta_ref.5) | copy-start | bytes 417796
  0.7 28.9 %copy-start.3 = (s32[4]{0:T(128)S(1)}, s32[4]{0:T(128)}, u32[]{:S(2)}) copy-start(s32[4]{0:T(128)} %count_ref.1) | copy-start | bytes 52
  0.7 28.9 %copy-start.2 = (f32[4,128,8]{1,2,0:T(8,128)S(1)}, f32[4,128,8]{1,2,0:T(8,128)}, u32[]{:S(2)}) copy-start(f32[4,128,8]{1,2,0:T(8,128)} %param.13) | copy-start | bytes 49156
  24.9 18.9 %all-to-all-start.1 = ((bf16[128,9,2,128]{3,2,1,0:T(2,128)(2,1)}), bf16[128,9,2,128]{3,2,1,0:T(2,128)(2,1)S(1)}, u32[]{:S(2)}, u32[]{:S(2)}) async-start(bf16[128,9,2,128]{3,2,1,0:T(2,128)(2,1)} %bitcast.3), calls=%async_computation.1 | async-start | bytes 1179648 | tf_op jit(solution)/shard_map/all_to_all | solution.py:330
  48.0 21.0 %all-to-all-start.2 = ((bf16[128,8,384]{2,1,0:T(8,128)(2,1)}), bf16[128,8,384]{2,1,0:T(8,128)(2,1)S(1)}, u32[]{:S(2)}, u32[]{:S(2)}) async-start(bf16[128,8,384]{2,1,0:T(8,128)(2,1)} %bitcast.8), calls=%async_computation.2 | async-start | bytes 1572864 | tf_op jit(solution)/shard_map/all_to_all | solution.py:330
  52.9 16.1 %copy-start = (bf16[1024,384]{1,0:T(8,128)(2,1)S(1)}, bf16[1024,384]{1,0:T(8,128)(2,1)}, u32[]{:S(2)}) copy-start(bf16[1024,384]{1,0:T(8,128)(2,1)} %refs_1_.3) | copy-start | bytes 2359300

commit v5 on v3

--- a/solution.py
+++ b/solution.py
@@ -10,7 +10,7 @@
 RANKS = 6
 ROWS = 8
 LANES = 128
-PRED_STRIDE = 48
+BIAS_ROWS = 4
 TILE = 256
 F32 = jnp.float32
 BF16 = jnp.bfloat16
@@ -173,6 +173,27 @@
     copy.wait()
 
 
+def reorder(ref, table, group, turns):
+    count, profile = table.shape
+    cuts = profile // LANES
+    devices = count // RANKS
+    batch = 8
+
+    def turn(index, carry):
+        for g in range(devices // batch // turns):
+            at = index * (devices // batch // turns) + g
+            start = pl.multiple_of(at * batch * group, 16)
+            rows_in = ref[pl.ds(start, batch * group), :]
+            here = pl.ds(pl.multiple_of(at * batch * RANKS, 16), batch * RANKS)
+            for c in range(cuts):
+                first = [d * group + c * RANKS for d in range(batch)]
+                part = jnp.concatenate([rows_in[f : f + RANKS, :] for f in first], axis=0)
+                table[here, c * LANES : (c + 1) * LANES] = part
+        return carry
+
+    lax.fori_loop(0, turns, turn, 0)
+
+
 def main_kernel(
     arrived_ref,
     pos_ref,
@@ -185,21 +206,23 @@
     beta_ref,
     coef_hbm,
     out_hbm,
+    left_hbm,
     left_ref,
     sums,
     turned,
-    placed,
+    wide,
     coef,
     out,
     table,
     chosen,
     coef_sem,
     out_sem,
+    left_sem,
 ):
     blocks, block_len = pos_ref.shape
-    rows, profile = out.shape
+    profile = coef.shape[0]
     npred, channels = sums.shape
-    devices = rows // ROWS
+    devices = turned.shape[0]
     cuts = profile // LANES
     share = channels // devices
     depth = norm_ref.shape[0]
@@ -208,38 +231,36 @@
 
     count = devices * RANKS
     group = RANKS * cuts
-    batch = 8
-    for g in range(devices // batch):
-        rows_in = arrived_ref[g * batch * group : (g + 1) * batch * group, :]
-        for c in range(cuts):
-            first = [d * group + c * RANKS for d in range(batch)]
-            part = jnp.concatenate([rows_in[f : f + RANKS, :] for f in first], axis=0)
-            here = slice(g * batch * RANKS, (g + 1) * batch * RANKS)
-            table[here, c * LANES : (c + 1) * LANES] = part
+    reorder(arrived_ref, table, group, 2)
+    below = []
     for k in range(blocks):
         here = pl.ds(k * block_len, block_len)
         row = pos_ref[k : k + 1, :]
         owner = lax.shift_right_arithmetic(row, ROWS.bit_length() - 1)
+        below.append(jnp.where(row < 0, -1, (row & (ROWS - 1)) * devices + owner))
         row = jnp.where(row < 0, -1, row - owner * (ROWS - RANKS))
         column = jnp.broadcast_to(row.astype(F32), (block_len, block_len)).T.astype(jnp.int32)
         lane = iota((block_len, count), 1)
         chosen[here, :] = one_hot(jnp.concatenate([column] * (count // block_len), axis=1) == lane)
     left_ref[:, 0:profile] = dot(chosen[...], table[...]).astype(BF16)
     left_ref[:, profile:] = side_ref[...]
+    left_copy = pltpu.make_async_copy(left_ref, left_hbm, left_sem)
+    left_copy.start()
     left = left_ref[:, 0:depth]
 
     pulled = dot(left, norm_ref[...])
     pulled = (pulled[:, 0:profile] + pulled[:, profile:] - base_ref[...]).astype(BF16)
-    step = rows // out_sem.shape[0]
-
-    def copy(t):
-        cut = pl.ds(t * step, step)
-        return pltpu.make_async_copy(out.at[cut], out_hbm.at[cut], out_sem.at[t])
-
-    for k in range(0, rows, step):
+    chunk = group + BIAS_ROWS
+    step = 256
+    for k in range(0, count, step):
         index = iota((step, block_len), 0) + k
-        place = [one_hot(index == pos_ref[b : b + 1, :]) for b in range(blocks)]
-        placed[k : k + step, :] = dot(jnp.concatenate(place, axis=1), pulled)
+        place = jnp.concatenate([one_hot(index == row) for row in below], axis=1)
+        placed = dot(place, pulled)
+        for r in range(k // devices, (k + step) // devices):
+            for c in range(cuts):
+                wide[pl.ds(c * RANKS + r, devices, stride=chunk), :] = placed[
+                    r * devices - k : (r + 1) * devices - k, c * LANES : (c + 1) * LANES
+                ]
 
     mixed = dot(stack_ref[...], left)
     high, low = split(mixed[0:npred] + mixed[npred:])
@@ -250,25 +271,18 @@
     sums[...] = weight_ref[...] * (mixed[0:npred] + mixed[npred:] - sums_ref[...])
     for d in range(devices):
         turned[d, :, 0:share] = sums[:, d * share : (d + 1) * share]
-    bias = jnp.concatenate(
-        [
-            jnp.concatenate(
-                [turned[:, p, 0:share], jnp.zeros((devices, PRED_STRIDE - share), F32)], axis=1
-            )
-            for p in range(npred)
-        ],
-        axis=1,
-    )
-    bias = jnp.concatenate(split(bias), axis=0)
-    for k in range(0, rows, step):
-        device = iota((step, devices), 1) * ROWS
-        index = iota((step, devices), 0) + k
-        place = [one_hot(index == device + (ROWS - 2)), one_hot(index == device + (ROWS - 1))]
-        extra = dot(jnp.concatenate(place, axis=1), bias)
-        out[k : k + step, :] = (placed[k : k + step, :] + extra).astype(BF16)
-        copy(k // step).start()
-    for k in range(rows // step):
-        copy(k).wait()
+    bias = jnp.concatenate([turned[:, p, 0:share] for p in range(npred)], axis=1)
+    high = bias.astype(BF16).astype(F32)
+    spare = BIAS_ROWS * LANES - npred * share
+    both = jnp.concatenate([high, (bias - high)[:, 0:spare]], axis=1)
+    for q in range(BIAS_ROWS):
+        part = both[:, q * LANES : (q + 1) * LANES]
+        wide[pl.ds(group + q, devices, stride=chunk), :] = part
+    out[...] = wide[...].astype(BF16)
+    copy = pltpu.make_async_copy(out, out_hbm, out_sem)
+    copy.start()
+    left_copy.wait()
+    copy.wait()
 
 
 def radiance_kernel(left_ref, beta_ref, coef_hbm, out_hbm, out, coef, sem, coef_sem):
@@ -294,29 +308,51 @@
         copy(t).wait()
 
 
-def final_kernel(ids_ref, base_ref, back_ref, grad_ref, bias_ref, *, scaling):
+def groups_of(shape, dim, size):
+    index = iota(shape, dim)
+    group = jnp.floor((index.astype(F32) + 0.5) * (1.0 / size)).astype(jnp.int32)
+    return group, index - group * size
+
+
+def target_kernel(ids_ref, after_ref, place_ref):
     devices = ids_ref.shape[0]
-    columns = base_ref.shape[0]
-    rows = back_ref.shape[0]
-    npred, share = bias_ref.shape
+    columns, count = place_ref.shape
     by_row = ids_ref[...].astype(F32).T[0:ROWS, :].astype(jnp.int32) + 1
     halves = jnp.concatenate(
         [lax.shift_right_logical(by_row, 5).astype(F32), (by_row & 31).astype(F32)], axis=0
     ).astype(BF16)
-    spread = one_hot(lax.shift_right_logical(iota((devices, rows), 1), 3) == iota((devices, rows), 0))
-    both = dot(halves, spread)
+    owner, _ = groups_of((devices, count), 1, RANKS)
+    both = dot(halves, one_hot(owner == iota((devices, count), 0)))
     both = both[0:ROWS] * 32.0 + both[ROWS:]
-    mine = (iota((ROWS, rows), 1) & (ROWS - 1)) == iota((ROWS, rows), 0)
+    _, rank = groups_of((ROWS, count), 1, RANKS)
+    mine = rank == iota((ROWS, count), 0)
     wanted = jnp.sum(jnp.where(mine, both, 0.0), axis=0, keepdims=True).astype(jnp.int32) - 1
     step = 256
     for k in range(0, columns, step):
-        place = one_hot(iota((step, rows), 0) + k == wanted)
+        place_ref[k : k + step, :] = one_hot(iota((step, count), 0) + k == wanted)
+
+
+def final_kernel(place_ref, base_ref, back_ref, grad_ref, bias_ref, table, *, scaling):
+    columns, count = place_ref.shape
+    devices = count // RANKS
+    rows = back_ref.shape[0]
+    chunk = rows // devices
+    npred, share = bias_ref.shape
+    _, inside = groups_of((ROWS, rows), 1, chunk)
+    last = one_hot(inside == iota((ROWS, rows), 0) + (chunk - BIAS_ROWS))
+    total = dot(last, back_ref[...])
+    total = jnp.concatenate([total[q : q + 1, :] for q in range(BIAS_ROWS)], axis=1)
+    high, low = total[:, 0 : npred * share], total[:, npred * share :]
+    spare = npred * share - low.shape[1]
+    total = (high + jnp.concatenate([low, jnp.zeros((1, spare), F32)], axis=1)) * scaling
+    for p in range(npred):
+        bias_ref[p : p + 1, :] = total[:, p * share : (p + 1) * share]
+    reorder(back_ref, table, chunk, 1)
+    step = 256
+    for k in range(0, columns, step):
         jacobian = 1.0 + 0.5 * jnp.tanh(base_ref[k : k + step, :].astype(F32))
-        grad_ref[k : k + step, :] = (dot(place, back_ref[...]) * jacobian).astype(BF16)
-    last = one_hot((iota((ROWS, rows), 1) & (ROWS - 1)) >= ROWS - 2)
-    total = dot(last, back_ref[...])[0:1, :] * scaling
-    for p in range(npred):
-        bias_ref[p : p + 1, :] = total[:, p * PRED_STRIDE : p * PRED_STRIDE + share]
+        grad = dot(place_ref[k : k + step, :], table[...]) * jacobian
+        grad_ref[k : k + step, :] = grad.astype(BF16)
 
 
 def exchange(x):
@@ -340,12 +376,12 @@
     channels = coefficients.shape[1]
     npred = bias_pred.shape[2]
     slots = blocks * block_len
-    rows = devices * ROWS
     shift = columns.bit_length() - 1
     assert columns == 1 << shift and channels % (TILE * 1) == 0
     scaling = float((slots * devices) ** -0.5)
     depth = profile + 4 * npred
     group = RANKS * profile // LANES
+    chunk = group + BIAS_ROWS
 
     def shape(*dims, dtype=BF16):
         return jax.ShapeDtypeStruct(dims, dtype)
@@ -438,25 +474,39 @@
     )
     outgoing, left = call(
         main_kernel,
-        (shape(rows, profile), shape(slots, profile + LANES)),
+        (
+            shape(devices * chunk, LANES),
+            pltpu.HBM((slots, profile + LANES), BF16),
+        ),
         (arrived, slot_pos, side, stack, norm, base, weight, base_sums, beta_incr, coef_hbm),
         2e9,
         in_specs=[VMEM] * 9 + [ANY],
-        out_specs=(ANY, VMEM),
+        out_specs=(ANY, ANY),
         scratch=[
+            pltpu.VMEM((slots, profile + LANES), BF16),
             pltpu.VMEM((npred, channels), F32),
             pltpu.VMEM((devices, npred, LANES), F32),
-            pltpu.VMEM((rows, profile), F32),
+            pltpu.VMEM((devices * chunk, LANES), F32),
             pltpu.VMEM((profile, channels), BF16),
-            pltpu.VMEM((rows, profile), BF16),
+            pltpu.VMEM((devices * chunk, LANES), BF16),
             pltpu.VMEM((devices * RANKS, profile), BF16),
             pltpu.VMEM((slots, devices * RANKS), BF16),
             pltpu.SemaphoreType.DMA,
-            pltpu.SemaphoreType.DMA((4,)),
+            pltpu.SemaphoreType.DMA,
+            pltpu.SemaphoreType.DMA,
         ],
         vmem=24,
     )
-    returned = exchange(outgoing.reshape(devices, ROWS, profile)).reshape(rows, profile)
+    returned = exchange(outgoing.reshape(devices, chunk // 2, 2, LANES))
+    returned = returned.reshape(devices * chunk, LANES)
+    place = call(
+        target_kernel,
+        shape(columns, devices * RANKS),
+        (ids, in_hbm(left)),
+        1e9,
+        in_specs=[VMEM, ANY],
+        vmem=16,
+    )
     radiance = call(
         radiance_kernel,
         shape(slots, channels),
@@ -475,8 +525,9 @@
     column_grad, bias_grad = call(
         lambda *refs: final_kernel(*refs, scaling=scaling),
         (shape(columns, profile), shape(npred, channels // devices, dtype=F32)),
-        (ids, background, returned),
+        (place, background, returned),
         1e9,
+        scratch=[pltpu.VMEM((devices * RANKS, profile), BF16)],
         vmem=16,
     )
     return (

time: 73.3 us -> 70.5 us (0.962)
  waiting for transfers between devices: 16.2 us -> 13.8 us
  Pallas kernels: 26 us -> 24.5 us
  local copies, waits for them, and re-layouts: 0.04 us -> 1.07 us
    all_to_all x2, waiting for transfers between devices: 16.2 us -> 13.8 us  [exchange(): return lax.all_to_all(x, AXES, split_axis=0, concat_axis=0, tiled=True)]
    pallas_call x6 -> x7, Pallas kernels: 26 us -> 24.5 us  [call(): pl.pallas_call(kernel, out_shape=outs, in_specs=in_specs or [VMEM] * len(...]
    unnamed x10 -> x12, local copies, waits for them, and re-layouts: 0.02 us -> 1.06 us
  transfers between devices with their start and end apart: 2 -> 2, of which waited for: 2 -> 2; matrix products, arithmetic and copies ran while one was open for 0% -> 0% of each run, Pallas kernels for 19% -> 21%
where the time goes in v5:
time: 70.5 us; the launch traced here: 70.1 us
  Pallas kernels  24.5 us (35%)
  blocking collectives  20.5 us (29%)
  waiting for transfers between devices  13.8 us (20%)
  starting transfers between devices  9.46 us (13%)
  local copies, waits for them, and re-layouts  1.07 us (2%)
  between operations  0.78 us (1%)
    pallas_call x7, Pallas kernels, call(): pl.pallas_call(kernel, out_shape=outs, in_specs=in_specs or [VMEM] * len(...  24.5 us
    all_to_all x1, blocking collectives, exchange(): return lax.all_to_all(x, AXES, split_axis=0, concat_axis=0, tiled=True)  20.5 us
    all_to_all x2, waiting for transfers between devices, exchange(): return lax.all_to_all(x, AXES, split_axis=0, concat_axis=0, tiled=True)  13.8 us
    all_to_all x2, starting transfers between devices, exchange(): return lax.all_to_all(x, AXES, split_axis=0, concat_axis=0, tiled=True)  9.46 us
  transfers between devices with their start and end apart: 2, of which 2 were waited for; matrix products, arithmetic and copies ran while one was open for 0% of the time, Pallas kernels for 21%

profile of v5, /device:TPU:0, one launch (start us, length us, event | category | flops | bytes accessed | tf_op | source)
XLA Modules:
  0.0 70.1 jit_solution(2709187098938666865)
XLA Ops:
  0.6 0.0 copy-start.5
  0.6 0.0 copy-start.1
  0.7 0.0 copy-start.3
  0.7 0.0 copy-start.2
  0.7 1.8 %shard_map.112 = (s32[128,128]{1,0:T(8,128)S(1)}, s32[4,128]{1,0:T(4,128)S(1)}, bf16[1024,384]{1,0:T(8,128)(2,1)S(1)}) custom-call(s32[4,128]{1,0:T(4,128)} %refs_0_.1, bf16[1024,384]{1,0:T(8,128)(2,1)} %refs_1_.3, bf16[1024,384]{1,0:T(8,128)(2,1)} %refs_2_.1), custom_call_target="tpu_custom_call" | custom-call | flops 100000000 | bytes 4194304 | tf_op jit(solution)/shard_map/pallas_call | solution.py:390
  2.5 20.5 %all_to_all.15 = s32[128,1,128]{2,1,0:T(1,128)S(1)} all-to-all(s32[128,1,128]{2,1,0:T(1,128)S(1)} %bitcast.17), channel_id=1, replica_groups=mesh['lat_0'=4,'lat_1'=2,'lon_0'=4,'lon_1'=4] {'lat_0','lat_1','lon_0','..., dimensions={0} | all-to-all | bytes 131072 | tf_op jit(solution)/shard_map/all_to_all | solution.py:359
  23.0 1.9 %shard_map.113 = bf16[2304,128]{1,0:T(8,128)(2,1)} custom-call(s32[128,128]{1,0:T(8,128)S(1)} %bitcast.14, bf16[1024,384]{1,0:T(8,128)(2,1)S(1)} %get-tuple-element.20.form_ref), custom_call_target="tpu_custom_call" | custom-call | flops 1000000000 | bytes 4194304 | tf_op jit(solution)/shard_map/pallas_call | solution.py:390
  24.9 4.6 %all-to-all-start.1 = ((bf16[128,9,2,128]{3,2,1,0:T(2,128)(2,1)}), bf16[128,9,2,128]{3,2,1,0:T(2,128)(2,1)S(1)}, u32[]{:S(2)}, u32[]{:S(2)}) async-start(bf16[128,9,2,128]{3,2,1,0:T(2,128)(2,1)} %bitcast.3), calls=%async_computation.1 | async-start | bytes 1179648 | tf_op jit(solution)/shard_map/all_to_all | solution.py:359
  29.5 0.0 copy-done.5
  29.6 0.0 copy-done.1
  29.6 0.0 copy-done.3
  29.6 0.0 copy-done.2
  29.6 8.6 %shard_map.114 = (s32[4,128]{1,0:T(4,128)S(1)}, bf16[416,768]{1,0:T(8,128)(2,1)S(1)}, f32[512,384]{1,0:T(8,128)S(1)}, f32[8,4352]{1,0:T(8,128)S(1)}, bf16[512,12...) custom-call(s32[128,128]{1,0:T(8,128)S(1)} %bitcast.15, s32[4,128]{1,0:T(4,128)S(1)} %get-tuple-element.21.pos_ref, ...), custom_call_target="tpu_custom_call" | custom-call | flops 8000000000 | bytes 4194304 | tf_op jit(solution)/shard_map/pallas_call | solution.py:390
  38.2 5.6 %all-to-all-done.1 = bf16[128,9,2,128]{3,2,1,0:T(2,128)(2,1)S(1)} async-done(((bf16[128,9,2,128]{3,2,1,0:T(2,128)(2,1)}), bf16[128,9,2,128]{3,2,1,0:T(2,128)(2,1)S(1)}, u32[]{:S(2)}, u32[]{:S(2)}) %all-to-all-start.1) | async-done | bytes 589856 | tf_op jit(solution)/shard_map/all_to_all | solution.py:359
  43.8 3.9 %shard_map.115 = (bf16[2816,128]{1,0:T(8,128)(2,1)}, bf16[512,512]{1,0:T(8,128)(2,1)}) custom-call(bf16[2304,128]{1,0:T(8,128)(2,1)S(1)} %bitcast.13, s32[4,128]{1,0:T(4,128)S(1)} %get-tuple-element.23.pos_ref, bf16[512,128]{1,0:T(8,128)(2,1)S(1)} %get-tuple-element.24.side_ref, bf16[16,512]{1,0:T(8,128)(2,1)S(1)} %get-tuple-element.25.stack_ref, ...), custom_call_target="tpu_custom_call" | custom-call | flops 2000000000 | bytes 4194304 | tf_op jit(solution)/shard_map/pallas_call | solution.py:390
  47.7 4.8 %all-to-all-start.2 = ((bf16[128,11,2,128]{3,2,1,0:T(2,128)(2,1)}), bf16[128,11,2,128]{3,2,1,0:T(2,128)(2,1)S(1)}, u32[]{:S(2)}, u32[]{:S(2)}) async-start(bf16[128,11,2,128]{3,2,1,0:T(2,128)(2,1)} %bitcast.8), calls=%async_computation.2 | async-start | bytes 1441792 | tf_op jit(solution)/shard_map/all_to_all | solution.py:359
  52.6 0.7 %shard_map.117.refs_0_ = bf16[1024,768]{1,0:T(8,128)(2,1)S(1)} custom-call(s32[128,128]{1,0:T(8,128)S(1)} %bitcast.16, bf16[512,512]{1,0:T(8,128)(2,1)} %get-tuple-element.29.left_ref.after_ref), custom_call_target="tpu_custom_call" | custom-call | flops 1000000000 | bytes 4194304 | tf_op jit(solution)/shard_map/pallas_call | solution.py:390
  53.3 0.0 copy-start.4
  53.3 1.0 %copy-done.4 = bf16[512,512]{1,0:T(8,128)(2,1)S(1)} copy-done((bf16[512,512]{1,0:T(8,128)(2,1)S(1)}, bf16[512,512]{1,0:T(8,128)(2,1)}, u32[]{:S(2)}) %copy-start.4) | copy-done | bytes 524312
  54.4 0.0 copy-start
  54.4 5.5 %shard_map.116 = bf16[512,4352]{1,0:T(8,128)(2,1)} custom-call(bf16[512,512]{1,0:T(8,128)(2,1)S(1)} %copy-done.4, f32[8,4352]{1,0:T(8,128)S(1)} %copy-done.1, bf16[384,4352]{1,0:T(8,128)(2,1)} %coef_hbm.5), custom_call_target="tpu_custom_call" | custom-call | flops 3000000000 | bytes 4194304 | tf_op jit(solution)/shard_map/pallas_call | solution.py:390
  59.9 8.2 %all-to-all-done.2 = bf16[128,11,2,128]{3,2,1,0:T(2,128)(2,1)S(1)} async-done(((bf16[128,11,2,128]{3,2,1,0:T(2,128)(2,1)}), bf16[128,11,2,128]{3,2,1,0:T(2,128)(2,1)S(1)}, u32[]{:S(2)}, u32[]{:S(2)}) %all-to-all-start.2) | async-done | bytes 720928 | tf_op jit(solution)/shard_map/all_to_all | solution.py:359
  68.0 0.0 copy-done
  68.0 2.1 %shard_map.118 = (bf16[1024,384]{1,0:T(8,128)(2,1)}, f32[8,34]{1,0:T(8,128)}) custom-call(bf16[1024,768]{1,0:T(8,128)(2,1)S(1)} %shard_map.117.refs_0_, bf16[1024,384]{1,0:T(8,128)(2,1)S(1)} %copy-done, bf16[2816,128]{1,0:T(8,128)(2,1)S(1)} %bitcast.12), custom_call_target="tpu_custom_call" | custom-call | flops 1000000000 | bytes 4194304 | tf_op jit(solution)/shard_map/pallas_call | solution.py:390
  (1 shorter events, 0.0 us)
Async XLA Ops:
  0.6 28.9 %copy-start.5 = (f32[4352]{0:T(1024)S(1)}, f32[4352]{0:T(1024)}, u32[]{:S(2)}) copy-start(f32[4352]{0:T(1024)} %param.15) | copy-start | bytes 52228
  0.6 28.9 %copy-start.1 = (f32[8,4352]{1,0:T(8,128)S(1)}, f32[8,4352]{1,0:T(8,128)}, u32[]{:S(2)}) copy-start(f32[8,4352]{1,0:T(8,128)} %beta_ref.5) | copy-start | bytes 417796
  0.7 28.9 %copy-start.3 = (s32[4]{0:T(128)S(1)}, s32[4]{0:T(128)}, u32[]{:S(2)}) copy-start(s32[4]{0:T(128)} %count_ref.1) | copy-start | bytes 52
  0.7 28.9 %copy-start.2 = (f32[4,128,8]{1,2,0:T(8,128)S(1)}, f32[4,128,8]{1,2,0:T(8,128)}, u32[]{:S(2)}) copy-start(f32[4,128,8]{1,2,0:T(8,128)} %param.13) | copy-start | bytes 49156
  24.9 18.9 %all-to-all-start.1 = ((bf16[128,9,2,128]{3,2,1,0:T(2,128)(2,1)}), bf16[128,9,2,128]{3,2,1,0:T(2,128)(2,1)S(1)}, u32[]{:S(2)}, u32[]{:S(2)}) async-start(bf16[128,9,2,128]{3,2,1,0:T(2,128)(2,1)} %bitcast.3), calls=%async_computation.1 | async-start | bytes 1179648 | tf_op jit(solution)/shard_map/all_to_all | solution.py:359
  47.7 20.3 %all-to-all-start.2 = ((bf16[128,11,2,128]{3,2,1,0:T(2,128)(2,1)}), bf16[128,11,2,128]{3,2,1,0:T(2,128)(2,1)S(1)}, u32[]{:S(2)}, u32[]{:S(2)}) async-start(bf16[128,11,2,128]{3,2,1,0:T(2,128)(2,1)} %bitcast.8), calls=%async_computation.2 | async-start | bytes 1441792 | tf_op jit(solution)/shard_map/all_to_all | solution.py:359
  53.3 1.0 %copy-start.4 = (bf16[512,512]{1,0:T(8,128)(2,1)S(1)}, bf16[512,512]{1,0:T(8,128)(2,1)}, u32[]{:S(2)}) copy-start(bf16[512,512]{1,0:T(8,128)(2,1)} %get-tuple-element.29.left_ref.after_ref) | copy-start | bytes 1572868
  54.4 13.6 %copy-start = (bf16[1024,384]{1,0:T(8,128)(2,1)S(1)}, bf16[1024,384]{1,0:T(8,128)(2,1)}, u32[]{:S(2)}) copy-start(bf16[1024,384]{1,0:T(8,128)(2,1)} %refs_1_.3) | copy-start | bytes 2359300

commit v6 on v5

--- a/solution.py
+++ b/solution.py
@@ -39,12 +39,15 @@
 def index_kernel(
     col_hbm, base_hbm, step_hbm, req_ref, pos_ref, form_ref, col_ref, base_ref, step_ref, sem, *, shift
 ):
-    copies = [
-        pltpu.make_async_copy(source, target, sem.at[k])
-        for k, (source, target) in enumerate(
-            [(col_hbm, col_ref), (base_hbm, base_ref), (step_hbm, step_ref)]
-        )
-    ]
+    parts = (sem.shape[0] - 1) // 2
+    size = base_ref.shape[0] // parts
+    copies = [pltpu.make_async_copy(col_hbm, col_ref, sem.at[0])]
+    for t in range(parts):
+        cut = pl.ds(t * size, size)
+        copies += [
+            pltpu.make_async_copy(base_hbm.at[cut], base_ref.at[cut], sem.at[2 * t + 1]),
+            pltpu.make_async_copy(step_hbm.at[cut], step_ref.at[cut], sem.at[2 * t + 2]),
+        ]
     for copy in copies:
         copy.start()
     copies[0].wait()
@@ -73,10 +76,12 @@
     low = jnp.concatenate(low, axis=1).astype(BF16)
     nt = ((1,), (1,))
     req_ref[...] = (dot(table, high, nt) * 32.0 + dot(table, low, nt)).astype(jnp.int32) - 1
-    copies[1].wait()
-    copies[2].wait()
-    jacobian = 1.0 + 0.5 * jnp.tanh(base_ref[...].astype(F32))
-    form_ref[...] = (step_ref[...].astype(F32) * jacobian).astype(BF16)
+    for t in range(parts):
+        copies[2 * t + 1].wait()
+        copies[2 * t + 2].wait()
+        cut = slice(t * size, (t + 1) * size)
+        jacobian = 1.0 + 0.5 * jnp.tanh(base_ref[cut, :].astype(F32))
+        form_ref[cut, :] = (step_ref[cut, :].astype(F32) * jacobian).astype(BF16)
 
 
 def beta_rows(beta):
@@ -153,6 +158,17 @@
     sums_ref[...] = sums[0:npred] + sums[npred:]
 
 
+def store_halves(wide, out, out_hbm, sem):
+    half = out.shape[0] // 2
+    copies = []
+    for t in range(2):
+        cut = pl.ds(t * half, half)
+        out[cut, :] = wide[cut, :].astype(BF16)
+        copies.append(pltpu.make_async_copy(out.at[cut], out_hbm.at[cut], sem.at[t]))
+        copies[t].start()
+    return copies
+
+
 def owner_kernel(ids_ref, form_ref, out_hbm, pick, wide, out, sem):
     devices = ids_ref.shape[0]
     columns, profile = form_ref.shape
@@ -167,10 +183,9 @@
             wide[pl.ds(c * RANKS + r, devices, stride=group), :] = result[
                 r * devices : (r + 1) * devices, c * LANES : (c + 1) * LANES
             ]
-    out[...] = wide[...].astype(BF16)
-    copy = pltpu.make_async_copy(out, out_hbm, sem)
-    copy.start()
-    copy.wait()
+    copies = store_halves(wide, out, out_hbm, sem)
+    for copy in copies:
+        copy.wait()
 
 
 def reorder(ref, table, group, turns):
@@ -252,6 +267,7 @@
     pulled = (pulled[:, 0:profile] + pulled[:, profile:] - base_ref[...]).astype(BF16)
     chunk = group + BIAS_ROWS
     step = 256
+    coef_copy.wait()
     for k in range(0, count, step):
         index = iota((step, block_len), 0) + k
         place = jnp.concatenate([one_hot(index == row) for row in below], axis=1)
@@ -266,7 +282,6 @@
     high, low = split(mixed[0:npred] + mixed[npred:])
     mixed = jnp.concatenate([high.astype(F32), low.astype(F32)], axis=0).astype(BF16)
     tail = beta_rows(beta_ref[...])
-    coef_copy.wait()
     mixed = dot(mixed, jnp.concatenate([coef[...], tail, tail], axis=0))
     sums[...] = weight_ref[...] * (mixed[0:npred] + mixed[npred:] - sums_ref[...])
     for d in range(devices):
@@ -278,11 +293,9 @@
     for q in range(BIAS_ROWS):
         part = both[:, q * LANES : (q + 1) * LANES]
         wide[pl.ds(group + q, devices, stride=chunk), :] = part
-    out[...] = wide[...].astype(BF16)
-    copy = pltpu.make_async_copy(out, out_hbm, out_sem)
-    copy.start()
-    left_copy.wait()
-    copy.wait()
+    copies = store_halves(wide, out, out_hbm, out_sem)
+    for copy in copies + [left_copy]:
+        copy.wait()
 
 
 def radiance_kernel(left_ref, beta_ref, coef_hbm, out_hbm, out, coef, sem, coef_sem):
@@ -418,7 +431,7 @@
             pltpu.VMEM((blocks, block_len), jnp.int32),
             pltpu.VMEM((columns, profile), BF16),
             pltpu.VMEM((columns, profile), BF16),
-            pltpu.SemaphoreType.DMA((3,)),
+            pltpu.SemaphoreType.DMA((9,)),
         ],
         vmem=16,
     )
@@ -435,7 +448,7 @@
             pltpu.VMEM((devices * RANKS, columns), BF16),
             pltpu.VMEM((devices * group, LANES), F32),
             pltpu.VMEM((devices * group, LANES), BF16),
-            pltpu.SemaphoreType.DMA,
+            pltpu.SemaphoreType.DMA((2,)),
         ],
         vmem=16,
     )
@@ -492,7 +505,7 @@
             pltpu.VMEM((devices * RANKS, profile), BF16),
             pltpu.VMEM((slots, devices * RANKS), BF16),
             pltpu.SemaphoreType.DMA,
-            pltpu.SemaphoreType.DMA,
+            pltpu.SemaphoreType.DMA((2,)),
             pltpu.SemaphoreType.DMA,
         ],
         vmem=24,

time: 70.5 us -> 71 us (level)
  no operation moved by 1% of the time
where the time goes in v6:
time: 71 us; the launch traced here: 70.6 us
  Pallas kernels  25.1 us (35%)
  blocking collectives  20.5 us (29%)
  waiting for transfers between devices  13.8 us (19%)
  starting transfers between devices  9.46 us (13%)
  local copies, waits for them, and re-layouts  1.07 us (2%)
  between operations  0.78 us (1%)
    pallas_call x7, Pallas kernels, call(): pl.pallas_call(kernel, out_shape=outs, in_specs=in_specs or [VMEM] * len(...  25.1 us
    all_to_all x1, blocking collectives, exchange(): return lax.all_to_all(x, AXES, split_axis=0, concat_axis=0, tiled=True)  20.5 us
    all_to_all x2, waiting for transfers between devices, exchange(): return lax.all_to_all(x, AXES, split_axis=0, concat_axis=0, tiled=True)  13.8 us
    all_to_all x2, starting transfers between devices, exchange(): return lax.all_to_all(x, AXES, split_axis=0, concat_axis=0, tiled=True)  9.46 us
  transfers between devices with their start and end apart: 2, of which 2 were waited for; matrix products, arithmetic and copies ran while one was open for 0% of the time, Pallas kernels for 21%

profile of v6, /device:TPU:0, one launch (start us, length us, event | category | flops | bytes accessed | tf_op | source)
XLA Modules:
  0.0 70.6 jit_solution(11284098113497967876)
XLA Ops:
  0.6 0.0 copy-start.5
  0.6 0.0 copy-start.1
  0.7 0.0 copy-start.3
  0.7 0.0 copy-start.2
  0.7 1.7 %shard_map.112 = (s32[128,128]{1,0:T(8,128)S(1)}, s32[4,128]{1,0:T(4,128)S(1)}, bf16[1024,384]{1,0:T(8,128)(2,1)S(1)}) custom-call(s32[4,128]{1,0:T(4,128)} %refs_0_.1, bf16[1024,384]{1,0:T(8,128)(2,1)} %refs_1_.3, bf16[1024,384]{1,0:T(8,128)(2,1)} %refs_2_.1), custom_call_target="tpu_custom_call" | custom-call | flops 100000000 | bytes 4194304 | tf_op jit(solution)/shard_map/pallas_call | solution.py:403
  2.4 20.5 %all_to_all.15 = s32[128,1,128]{2,1,0:T(1,128)S(1)} all-to-all(s32[128,1,128]{2,1,0:T(1,128)S(1)} %bitcast.17), channel_id=1, replica_groups=mesh['lat_0'=4,'lat_1'=2,'lon_0'=4,'lon_1'=4] {'lat_0','lat_1','lon_0','..., dimensions={0} | all-to-all | bytes 131072 | tf_op jit(solution)/shard_map/all_to_all | solution.py:372
  22.9 1.9 %shard_map.113 = bf16[2304,128]{1,0:T(8,128)(2,1)} custom-call(s32[128,128]{1,0:T(8,128)S(1)} %bitcast.14, bf16[1024,384]{1,0:T(8,128)(2,1)S(1)} %get-tuple-element.20.form_ref), custom_call_target="tpu_custom_call" | custom-call | flops 1000000000 | bytes 4194304 | tf_op jit(solution)/shard_map/pallas_call | solution.py:403
  24.7 4.6 %all-to-all-start.1 = ((bf16[128,9,2,128]{3,2,1,0:T(2,128)(2,1)}), bf16[128,9,2,128]{3,2,1,0:T(2,128)(2,1)S(1)}, u32[]{:S(2)}, u32[]{:S(2)}) async-start(bf16[128,9,2,128]{3,2,1,0:T(2,128)(2,1)} %bitcast.3), calls=%async_computation.1 | async-start | bytes 1179648 | tf_op jit(solution)/shard_map/all_to_all | solution.py:372
  29.4 0.0 copy-done.5
  29.4 0.0 copy-done.1
  29.4 0.0 copy-done.3
  29.4 0.0 copy-done.2
  29.4 8.6 %shard_map.114 = (s32[4,128]{1,0:T(4,128)S(1)}, bf16[416,768]{1,0:T(8,128)(2,1)S(1)}, f32[512,384]{1,0:T(8,128)S(1)}, f32[8,4352]{1,0:T(8,128)S(1)}, bf16[512,12...) custom-call(s32[128,128]{1,0:T(8,128)S(1)} %bitcast.15, s32[4,128]{1,0:T(4,128)S(1)} %get-tuple-element.21.pos_ref, ...), custom_call_target="tpu_custom_call" | custom-call | flops 8000000000 | bytes 4194304 | tf_op jit(solution)/shard_map/pallas_call | solution.py:403
  38.0 5.6 %all-to-all-done.1 = bf16[128,9,2,128]{3,2,1,0:T(2,128)(2,1)S(1)} async-done(((bf16[128,9,2,128]{3,2,1,0:T(2,128)(2,1)}), bf16[128,9,2,128]{3,2,1,0:T(2,128)(2,1)S(1)}, u32[]{:S(2)}, u32[]{:S(2)}) %all-to-all-start.1) | async-done | bytes 589856 | tf_op jit(solution)/shard_map/all_to_all | solution.py:372
  43.6 4.6 %shard_map.115 = (bf16[2816,128]{1,0:T(8,128)(2,1)}, bf16[512,512]{1,0:T(8,128)(2,1)}) custom-call(bf16[2304,128]{1,0:T(8,128)(2,1)S(1)} %bitcast.13, s32[4,128]{1,0:T(4,128)S(1)} %get-tuple-element.23.pos_ref, bf16[512,128]{1,0:T(8,128)(2,1)S(1)} %get-tuple-element.24.side_ref, bf16[16,512]{1,0:T(8,128)(2,1)S(1)} %get-tuple-element.25.stack_ref, ...), custom_call_target="tpu_custom_call" | custom-call | flops 2000000000 | bytes 4194304 | tf_op jit(solution)/shard_map/pallas_call | solution.py:403
  48.3 4.8 %all-to-all-start.2 = ((bf16[128,11,2,128]{3,2,1,0:T(2,128)(2,1)}), bf16[128,11,2,128]{3,2,1,0:T(2,128)(2,1)S(1)}, u32[]{:S(2)}, u32[]{:S(2)}) async-start(bf16[128,11,2,128]{3,2,1,0:T(2,128)(2,1)} %bitcast.8), calls=%async_computation.2 | async-start | bytes 1441792 | tf_op jit(solution)/shard_map/all_to_all | solution.py:372
  53.1 0.7 %shard_map.117.refs_0_ = bf16[1024,768]{1,0:T(8,128)(2,1)S(1)} custom-call(s32[128,128]{1,0:T(8,128)S(1)} %bitcast.16, bf16[512,512]{1,0:T(8,128)(2,1)} %get-tuple-element.29.left_ref.after_ref), custom_call_target="tpu_custom_call" | custom-call | flops 1000000000 | bytes 4194304 | tf_op jit(solution)/shard_map/pallas_call | solution.py:403
  53.9 0.0 copy-start.4
  53.9 1.0 %copy-done.4 = bf16[512,512]{1,0:T(8,128)(2,1)S(1)} copy-done((bf16[512,512]{1,0:T(8,128)(2,1)S(1)}, bf16[512,512]{1,0:T(8,128)(2,1)}, u32[]{:S(2)}) %copy-start.4) | copy-done | bytes 524312
  54.9 0.0 copy-start
  54.9 5.5 %shard_map.116 = bf16[512,4352]{1,0:T(8,128)(2,1)} custom-call(bf16[512,512]{1,0:T(8,128)(2,1)S(1)} %copy-done.4, f32[8,4352]{1,0:T(8,128)S(1)} %copy-done.1, bf16[384,4352]{1,0:T(8,128)(2,1)} %coef_hbm.5), custom_call_target="tpu_custom_call" | custom-call | flops 3000000000 | bytes 4194304 | tf_op jit(solution)/shard_map/pallas_call | solution.py:403
  60.4 8.2 %all-to-all-done.2 = bf16[128,11,2,128]{3,2,1,0:T(2,128)(2,1)S(1)} async-done(((bf16[128,11,2,128]{3,2,1,0:T(2,128)(2,1)}), bf16[128,11,2,128]{3,2,1,0:T(2,128)(2,1)S(1)}, u32[]{:S(2)}, u32[]{:S(2)}) %all-to-all-start.2) | async-done | bytes 720928 | tf_op jit(solution)/shard_map/all_to_all | solution.py:372
  68.6 0.0 copy-done
  68.6 2.1 %shard_map.118 = (bf16[1024,384]{1,0:T(8,128)(2,1)}, f32[8,34]{1,0:T(8,128)}) custom-call(bf16[1024,768]{1,0:T(8,128)(2,1)S(1)} %shard_map.117.refs_0_, bf16[1024,384]{1,0:T(8,128)(2,1)S(1)} %copy-done, bf16[2816,128]{1,0:T(8,128)(2,1)S(1)} %bitcast.12), custom_call_target="tpu_custom_call" | custom-call | flops 1000000000 | bytes 4194304 | tf_op jit(solution)/shard_map/pallas_call | solution.py:403
  (1 shorter events, 0.0 us)
Async XLA Ops:
  0.6 28.8 %copy-start.5 = (f32[4352]{0:T(1024)S(1)}, f32[4352]{0:T(1024)}, u32[]{:S(2)}) copy-start(f32[4352]{0:T(1024)} %param.15) | copy-start | bytes 52228
  0.6 28.8 %copy-start.1 = (f32[8,4352]{1,0:T(8,128)S(1)}, f32[8,4352]{1,0:T(8,128)}, u32[]{:S(2)}) copy-start(f32[8,4352]{1,0:T(8,128)} %beta_ref.5) | copy-start | bytes 417796
  0.7 28.8 %copy-start.3 = (s32[4]{0:T(128)S(1)}, s32[4]{0:T(128)}, u32[]{:S(2)}) copy-start(s32[4]{0:T(128)} %count_ref.1) | copy-start | bytes 52
  0.7 28.8 %copy-start.2 = (f32[4,128,8]{1,2,0:T(8,128)S(1)}, f32[4,128,8]{1,2,0:T(8,128)}, u32[]{:S(2)}) copy-start(f32[4,128,8]{1,2,0:T(8,128)} %param.13) | copy-start | bytes 49156
  24.7 18.9 %all-to-all-start.1 = ((bf16[128,9,2,128]{3,2,1,0:T(2,128)(2,1)}), bf16[128,9,2,128]{3,2,1,0:T(2,128)(2,1)S(1)}, u32[]{:S(2)}, u32[]{:S(2)}) async-start(bf16[128,9,2,128]{3,2,1,0:T(2,128)(2,1)} %bitcast.3), calls=%async_computation.1 | async-start | bytes 1179648 | tf_op jit(solution)/shard_map/all_to_all | solution.py:372
  48.3 20.3 %all-to-all-start.2 = ((bf16[128,11,2,128]{3,2,1,0:T(2,128)(2,1)}), bf16[128,11,2,128]{3,2,1,0:T(2,128)(2,1)S(1)}, u32[]{:S(2)}, u32[]{:S(2)}) async-start(bf16[128,11,2,128]{3,2,1,0:T(2,128)(2,1)} %bitcast.8), calls=%async_computation.2 | async-start | bytes 1441792 | tf_op jit(solution)/shard_map/all_to_all | solution.py:372
  53.9 1.0 %copy-start.4 = (bf16[512,512]{1,0:T(8,128)(2,1)S(1)}, bf16[512,512]{1,0:T(8,128)(2,1)}, u32[]{:S(2)}) copy-start(bf16[512,512]{1,0:T(8,128)(2,1)} %get-tuple-element.29.left_ref.after_ref) | copy-start | bytes 1572868
  54.9 13.6 %copy-start = (bf16[1024,384]{1,0:T(8,128)(2,1)S(1)}, bf16[1024,384]{1,0:T(8,128)(2,1)}, u32[]{:S(2)}) copy-start(bf16[1024,384]{1,0:T(8,128)(2,1)} %refs_1_.3) | copy-start | bytes 2359300
